TPU v7x, 64 devices: a 2x2x8 block of a 4x4x8 slice. The times are simulated.
64 devices in a mesh: rep: 8 (over x, y, core), dp: 8 (over z).
Axes of the slice: x: 2, y: 2, z: 8, core: 2. Of those that a mesh axis runs over, the one named last changes fastest.
The devices are a block of a 4x4x8 slice.
Arguments:
- x: bfloat16 [64, 4096, 512], P(('rep', 'dp')), parts along dimension 0
- dy: bfloat16 [64, 4096, 512], P(('rep', 'dp')), parts along dimension 0
- w_gate: bfloat16 [2, 512, 1280], replicated
- w_up: bfloat16 [2, 512, 1280], replicated
- w_down: bfloat16 [2, 1280, 512], replicated
- m_w_gate: float32 [2, 512, 1280], P(None, 'dp')
- m_w_up: float32 [2, 512, 1280], P(None, 'dp')
- m_w_down: float32 [2, 1280, 512], P(None, 'dp')
- v_w_gate: float32 [2, 512, 1280], P(None, 'dp')
- v_w_up: float32 [2, 512, 1280], P(None, 'dp')
- v_w_down: float32 [2, 1280, 512], P(None, 'dp')
Outputs:
- output 1: bfloat16 [16, 512, 1280], P('rep'), parts along dimension 0
- output 2: bfloat16 [16, 512, 1280], P('rep'), parts along dimension 0
- output 3: bfloat16 [16, 1280, 512], P('rep'), parts along dimension 0
- output 4: float32 [16, 512, 1280], P('rep', 'dp'), parts along dimension 0
- output 5: float32 [16, 512, 1280], P('rep', 'dp'), parts along dimension 0
- output 6: float32 [16, 1280, 512], P('rep', 'dp'), parts along dimension 0
- output 7: float32 [16, 512, 1280], P('rep', 'dp'), parts along dimension 0
- output 8: float32 [16, 512, 1280], P('rep', 'dp'), parts along dimension 0
- output 9: float32 [16, 1280, 512], P('rep', 'dp'), parts along dimension 0
There are 8 independent parts. A program takes and returns all parts, laid end to end along the dimension named above; an argument that names none is the same for every part.
All inputs are finite; a program needn't handle non-finite values.
Results may differ from a plain program's by a relative error of at most 0.022.
Values are sent between devices in bfloat16 or wider.
A program may use at most 768 MiB of HBM per device.

v0:
```python
import jax
import jax.numpy as jnp
from jax import lax

NAMES = ("w_gate", "w_up", "w_down")


def matmul(a, w):
    return jnp.dot(a, w, preferred_element_type=jnp.float32).astype(jnp.bfloat16)


def normed(h):
    wide = h.astype(jnp.float32)
    scale = lax.rsqrt(jnp.mean(wide**2, -1, keepdims=True) + 1e-6)
    return (wide * scale).astype(jnp.bfloat16)


def layer(h, w):
    a = normed(h)
    gate = jnp.dot(a, w["w_gate"], preferred_element_type=jnp.float32)
    up = jnp.dot(a, w["w_up"], preferred_element_type=jnp.float32)
    return h + matmul((jax.nn.silu(gate) * up).astype(jnp.bfloat16), w["w_down"])


def adamw(w, m, v, g):
    m = 0.9 * m + 0.1 * g
    v = 0.95 * v + 0.05 * g * g
    step = m * lax.rsqrt(v + 1e-8) + 0.1 * w
    return (w - 0.02 * step).astype(jnp.bfloat16), m, v


def clipped(gradients, sum_of_squares, count):
    factor = jnp.minimum(1.0, 0.5 * lax.rsqrt(sum_of_squares / count + 1e-30))
    return [g * factor for g in gradients]


def stack(weights, h):
    for number in range(weights["w_gate"].shape[0]):
        h = layer(h, {name: w[number] for name, w in weights.items()})
    return h


def solution(mesh):
    groups = mesh.shape["rep"]

    def step(x, dy, *arrays):
        weights, m, v = (arrays[i : i + 3] for i in (0, 3, 6))
        x, dy = (t.reshape(groups, -1, *t.shape[1:]) for t in (x, dy))

        def of_a_group(x, dy):
            _, back = jax.vjp(lambda w: stack(w, x), dict(zip(NAMES, weights, strict=True)))
            by_weights = back(dy)[0]
            gradients = [by_weights[name].astype(jnp.float32) for name in NAMES]
            gradients = clipped(gradients, sum(jnp.sum(g * g) for g in gradients), sum(g.size for g in gradients))
            new = [adamw(w.astype(jnp.float32), m, v, g) for w, m, v, g in zip(weights, m, v, gradients, strict=True)]
            return tuple(one[which] for which in range(3) for one in new)

        return tuple(t.reshape(-1, *t.shape[2:]) for t in jax.vmap(of_a_group)(x, dy))

    return step
```

profile of v0, /device:TPU:22, one launch (start us, length us, event | category | flops | bytes accessed | tf_op | source)
XLA Modules:
  0.0 699.6 jit_solution(8477792311350579993)
XLA Ops:
  10.3 6.4 copy
  16.8 6.5 copy.1
  23.3 11.8 %fusion.168 = bf16[1,1,4096,1280]{3,2,1,0:T(8,128)(2,1)} fusion(bf16[1,4096,512]{2,1,0:T(8,128)(2,1)} %param.17, bf16[2,1280,512]{2,1,0:T(8,128)(2,1)S(1)} %copy-done.23), kind=kOutput, calls=%fused_computation.204 | convolution fusion | flops 5373952000 | bytes 15990784 | tf_op jit(solution)/vmap(transpose(jvp()))/dot_general | solution.py:9
  35.1 9.9 %fusion.210 = f32[4096,1280]{1,0:T(8,128)} fusion(bf16[1,4096,512]{2,1,0:T(8,128)(2,1)S(1)} %copy-done.5, f32[4096]{0:T(1024)S(1)} %add_rsqrt_fusion, bf16[2,512,1280]{2,1,0:T(8,128)(2,1)S(1)} %copy-done.25), kind=kOutput, calls=%fused_computation.235 | convolution fusion | flops 5375000576 | bytes 26492928 | tf_op jit(solution)/vmap(jvp())/dot_general | solution.py:20
  45.1 19.1 %fusion.164 = (bf16[1,1,4096,1280]{3,2,1,0:T(8,128)(2,1)}, f32[4096,1280]{1,0:T(8,128)}) fusion(f32[4096,1280]{1,0:T(8,128)} %fusion.210, bf16[2,512,1280]{2,1,0:T(8,128)(2,1)} %param.15, bf16[1,4096,512]{2,1,0:T(8,128)(2,1)} %param.14, f32[4096]{0:T(1024)S(1)} %add_rsqrt_fusion), kind=kOutput, calls=%fused_computation.191 | convolution fusion | flops 5406457856 | bytes 57950208 | tf_op jit(solution)/vmap(jvp())/dot_general | solution.py:21
  64.1 14.3 %copy.4 = bf16[1,1,4096,1280]{2,3,1,0:T(8,128)(2,1)} copy(bf16[1,1,4096,1280]{3,2,1,0:T(8,128)(2,1)} %get-tuple-element.263) | data formatting | bytes 20971520
  78.4 11.8 %fusion.176 = (f32[4096]{0:T(1024)S(1)}, bf16[1,1,4096,512]{2,3,1,0:T(8,128)(2,1)S(1)}) fusion(bf16[2,1280,512]{2,1,0:T(8,128)(2,1)S(1)} %copy-done.23, bf16[1,1,4096,1280]{3,2,1,0:T(8,128)(2,1)} %get-tuple-element.263, bf16[1,4096,512]{1,2,0:T(8,128)(2,1)} %copy), kind=kOutput, calls=%fused_computation.215 | convolution fusion | flops 5379190784 | bytes 20201472 | tf_op jit(solution)/vmap(jvp())/dot_general | solution.py:9
  95.1 10.0 %fusion.205 = f32[4096,1280]{1,0:T(8,128)} fusion(bf16[1,1,4096,512]{2,3,1,0:T(8,128)(2,1)S(1)} %fusion.177, bf16[2,512,1280]{2,1,0:T(8,128)(2,1)S(1)} %copy-done.24), kind=kOutput, calls=%fused_computation.231 | convolution fusion | flops 5368709120 | bytes 26476544 | tf_op jit(solution)/vmap(jvp())/dot_general | solution.py:21
  105.2 31.1 %fusion.153 = (bf16[1,1,4096,1280]{3,2,1,0:T(8,128)(2,1)}, bf16[1,1,4096,1280]{3,2,1,0:T(8,128)(2,1)}, f32[4096,1280]{1,0:T(8,128)}) fusion(f32[4096,1280]{1,0:T(8,128)} %fusion.205, bf16[1,1,4096,1280]{3,2,1,0:T(8,128)(2,1)} %fusion.168, bf16[2,512,1280]{2,1,0:T(8,128)(2,1)} %param.12, bf16[1,1,4096,512]{2,3,1,0:T(8,128)(2,1)} %copy-done), kind=kOutput, calls=%fused_computation.175 | convolution fusion | flops 5447352320 | bytes 78905344 | tf_op jit(solution)/vmap(jvp())/dot_general | solution.py:20
  136.3 11.6 %fusion.182 = bf16[4096,512]{0,1:T(8,128)(2,1)} fusion(bf16[1,1,4096,1280]{3,2,1,0:T(8,128)(2,1)} %get-tuple-element.622, bf16[2,512,1280]{2,1,0:T(8,128)(2,1)} %param.15), kind=kOutput, calls=%fused_computation.220 | convolution fusion | flops 5368709120 | bytes 15990784 | tf_op jit(solution)/vmap(transpose(jvp()))/dot_general | solution.py:21
  147.9 8.4 %fusion.178 = (f32[4096]{0:T(1024)S(1)}, bf16[1,1,4096,512]{2,3,1,0:T(8,128)(2,1)S(1)}) fusion(bf16[1,1,4096,512]{2,3,1,0:T(8,128)(2,1)S(1)} %copy-done.7, bf16[4096,512]{0,1:T(8,128)(2,1)} %fusion.182, bf16[2,512,1280]{2,1,0:T(8,128)(2,1)} %param.12, bf16[1,1,4096,1280]{3,2,1,0:T(8,128)(2,1)S(1)} %copy-done.1), kind=kOutput, calls=%fused_computation.217 | convolution fusion | flops 5379190784 | bytes 24395776 | tf_op jit(solution)/vmap(transpose(jvp()))/dot_general | solution.py:20
  160.7 6.5 copy.5
  167.3 48.1 %while.17 = (bf16[1,1,4096,1280]{2,3,1,0:T(8,128)(2,1)}, bf16[1,1,4096,512]{3,2,1,0:T(8,128)(2,1)}, f32[1,160,512]{2,1,0:T(8,128)S(1)}, f32[1,160,512]{2,1,0:T(8...) while((bf16[1,1,4096,1280]{2,3,1,0:T(8,128)(2,1)}, ...), condition=%wide.windowed_dot_general_cond_rs.5.clone, body=%wide.windowed_dot_general_body_rs.5.clone.sunk | while | flops 2695331840 | bytes 89391824 | solution.py:9
  215.5 19.0 %fusion.163 = bf16[1,1,4096,1280]{3,2,1,0:T(8,128)(2,1)} fusion(f32[4096,1280]{1,0:T(8,128)} %fusion.205, f32[4096,1280]{1,0:T(8,128)} %get-tuple-element.267), kind=kLoop, calls=%fused_computation.189 | loop fusion | flops 31457280 | bytes 52428800 | tf_op jit(solution)/vmap(jvp())/convert_element_type | solution.py:22
  234.5 14.3 %copy.2 = bf16[1,1,4096,1280]{2,3,1,0:T(8,128)(2,1)} copy(bf16[1,1,4096,1280]{3,2,1,0:T(8,128)(2,1)} %fusion.163) | data formatting | bytes 20971520
  248.8 6.5 copy.3
  255.3 43.4 %while.16 = (bf16[1,1,4096,1280]{2,3,1,0:T(8,128)(2,1)}, bf16[1,1,4096,512]{3,2,1,0:T(8,128)(2,1)}, f32[1,160,512]{2,1,0:T(8,128)S(1)}, f32[1,160,512]{2,1,0:T(8...) while((bf16[1,1,4096,1280]{2,3,1,0:T(8,128)(2,1)}, ...), condition=%wide.windowed_dot_general_cond_rs.4.clone, body=%wide.windowed_dot_general_body_rs.4.clone.sunk | while | flops 2695331840 | bytes 89391824 | solution.py:9
  304.1 28.3 %convert_multiply_fusion = (bf16[1,1,4096,1280]{3,2,1,0:T(8,128)(2,1)}, bf16[1,1,4096,1280]{3,2,1,0:T(8,128)(2,1)}) fusion(f32[4096,1280]{1,0:T(8,128)} %fusion.210, f32[4096,1280]{1,0:T(8,128)} %get-tuple-element.264, bf16[2,1280,512]{2,1,0:T(8,128)(2,1)} %param.16, bf16[1,1,4096,512]{2,3,1,0:T(8,128)(2,1)} %fusion.200), kind=kOutput, calls=%fused_computation.170 | convolution fusion | flops 5452595200 | bytes 68419584 | tf_op jit(solution)/vmap(transpose(jvp()))/dot_general | solution.py:9
  332.4 49.5 %while.15 = (bf16[1,1,4096,512]{2,3,1,0:T(8,128)(2,1)}, bf16[1,1,4096,1280]{3,2,1,0:T(8,128)(2,1)}, f32[1,64,1280]{2,1,0:T(8,128)S(1)}, f32[1,64,1280]{2,1,0:T(8...) while((bf16[1,1,4096,512]{2,3,1,0:T(8,128)(2,1)}, ...), condition=%wide.windowed_dot_general_cond_rs.3.clone, body=%wide.windowed_dot_general_body_rs.3.clone.sunk | while | flops 2689040384 | bytes 41157220 | solution.py:21
  337.7 5.9 fusion.345
  382.6 49.4 %while.14 = (bf16[1,1,4096,512]{2,3,1,0:T(8,128)(2,1)}, bf16[1,1,4096,1280]{3,2,1,0:T(8,128)(2,1)}, f32[1,64,1280]{2,1,0:T(8,128)S(1)}, f32[1,64,1280]{2,1,0:T(8...) while((bf16[1,1,4096,512]{2,3,1,0:T(8,128)(2,1)}, ...), condition=%wide.windowed_dot_general_cond_rs.2.clone, body=%wide.windowed_dot_general_body_rs.2.clone.sunk | while | flops 2689040384 | bytes 41157220 | solution.py:21
  388.4 5.9 fusion.337
  413.5 5.9 fusion.337
  432.7 44.5 %while.13 = (bf16[1,1,4096,512]{2,3,1,0:T(8,128)(2,1)}, bf16[1,1,4096,1280]{3,2,1,0:T(8,128)(2,1)}, f32[1,64,1280]{2,1,0:T(8,128)S(1)}, f32[1,64,1280]{2,1,0:T(8...) while((bf16[1,1,4096,512]{2,3,1,0:T(8,128)(2,1)}, ...), condition=%wide.windowed_dot_general_cond_rs.1.clone, body=%wide.windowed_dot_general_body_rs.1.clone.sunk | while | flops 2689040384 | bytes 41157220 | solution.py:20
  460.3 5.9 fusion.329
  477.2 53.4 %while.12 = (bf16[1,1,4096,512]{2,3,1,0:T(8,128)(2,1)}, bf16[1,1,4096,1280]{3,2,1,0:T(8,128)(2,1)}, f32[1,64,1280]{2,1,0:T(8,128)S(1)}, f32[1,64,1280]{2,1,0:T(8...) while((bf16[1,1,4096,512]{2,3,1,0:T(8,128)(2,1)}, ...), condition=%wide.windowed_dot_general_cond_rs.clone, body=%wide.windowed_dot_general_body_rs.clone.sunk | while | flops 2689040384 | bytes 42467968 | solution.py:20
  483.4 5.9 fusion.321
  508.7 5.8 fusion.321
  549.0 15.3 %all-reduce.10 = f32[1]{0:T(128)} all-reduce(f32[1]{0:T(128)} %bitcast.39), channel_id=13, replica_groups=mesh['rep'=8,'dp'=8] {'dp'}, use_global_device_ids=true, to_apply=%region_3.4.clone | all-reduce | flops 1 | bytes 8 | tf_op jit(solution)/vmap()/reduce_sum | solution.py:54
  573.7 32.9 %all-gather.14.cloned.1.call-done = bf16[1,2,1280,512]{3,2,1,0:T(8,128)(2,1)} async-done(((bf16[1,2,160,512]{3,2,1,0:T(8,128)(2,1)}), bf16[1,2,1280,512]{3,2,1,0:T(8,128)(2,1)}) %all-gather.14.cloned.1.call-update) | async-done | bytes 2621456 | tf_op jit(solution)/reshape | solution.py:58
  606.7 39.9 %all-gather.12.cloned.1.call-done = bf16[1,2,512,1280]{3,2,1,0:T(8,128)(2,1)} async-done(((bf16[1,2,64,1280]{3,2,1,0:T(8,128)(2,1)}), bf16[1,2,512,1280]{3,2,1,0:T(8,128)(2,1)}) %all-gather.12.cloned.1.call-update) | async-done | bytes 2621456 | tf_op jit(solution)/reshape | solution.py:58
  646.5 39.9 %all-gather.10.cloned.1.call-done = bf16[1,2,512,1280]{3,2,1,0:T(8,128)(2,1)} async-done(((bf16[1,2,64,1280]{3,2,1,0:T(8,128)(2,1)}), bf16[1,2,512,1280]{3,2,1,0:T(8,128)(2,1)}) %all-gather.10.cloned.1.call-update) | async-done | bytes 2621456 | tf_op jit(solution)/reshape | solution.py:58
  (316 shorter events, 278.5 us)
Async XLA Ops:
  7.2 599.5 %all-gather.14.cloned.1.call-start = ((), (), s32[]{:S(2)}) async-start(), calls=%async_computation.2 | async-start | bytes 2949120 | tf_op jit(solution)/reshape | solution.py:58
  167.3 15.2 %collective-permute-start.20 = (f32[1,160,512]{2,1,0:T(8,128)S(1)}, f32[1,160,512]{2,1,0:T(8,128)S(1)}, u32[]{:S(2)}, u32[]{:S(2)}) collective-permute-start(f32[1,160,512]{2,1,0:T(8,128)S(1)} %broadcast_select_fusion.34), channel_id=35, source_target_pairs={{0,1},{1,2},{2,3},{3,4},{4,5},{5,6},{6,7},{7,0},{8,9},{9,10},{10,1... | collective-permute-start | bytes 983048 | tf_op jit(solution)/vmap(transpose(jvp()))/dot_general | solution.py:9
  169.6 12.9 %collective-permute-start.21 = (f32[1,160,512]{2,1,0:T(8,128)S(1)}, f32[1,160,512]{2,1,0:T(8,128)S(1)}, u32[]{:S(2)}, u32[]{:S(2)}) collective-permute-start(f32[1,160,512]{2,1,0:T(8,128)S(1)} %broadcast_select_fusion.35), channel_id=34, source_target_pairs={{0,7},{1,0},{2,1},{3,2},{4,3},{5,4},{6,5},{7,6},{8,15},{9,8},{10,9... | collective-permute-start | bytes 983048 | tf_op jit(solution)/vmap(transpose(jvp()))/dot_general | solution.py:9
  215.3 316.9 %collective-permute-start.29 = (f32[1,160,512]{2,1,0:T(8,128)}, f32[1,160,512]{2,1,0:T(8,128)}, u32[]{:S(2)}, u32[]{:S(2)}) collective-permute-start(f32[1,160,512]{2,1,0:T(8,128)} %get-tuple-element.47), channel_id=38, source_target_pairs={{0,1},{1,2},{2,3},{3,4},{4,5},{5,6},{6,7},{7,0},{8,9},{9,10},{10,1... | collective-permute-start | bytes 983048 | tf_op jit(solution)/vmap(transpose(jvp()))/dot_general | solution.py:9
  255.4 10.7 %collective-permute-start.16 = (f32[1,160,512]{2,1,0:T(8,128)S(1)}, f32[1,160,512]{2,1,0:T(8,128)S(1)}, u32[]{:S(2)}, u32[]{:S(2)}) collective-permute-start(f32[1,160,512]{2,1,0:T(8,128)S(1)} %broadcast_select_fusion.32), channel_id=29, source_target_pairs={{0,1},{1,2},{2,3},{3,4},{4,5},{5,6},{6,7},{7,0},{8,9},{9,10},{10,1... | collective-permute-start | bytes 983048 | tf_op jit(solution)/vmap(transpose(jvp()))/dot_general | solution.py:9
  276.7 10.7 %collective-permute-start.16 = (f32[1,160,512]{2,1,0:T(8,128)S(1)}, f32[1,160,512]{2,1,0:T(8,128)S(1)}, u32[]{:S(2)}, u32[]{:S(2)}) collective-permute-start(f32[1,160,512]{2,1,0:T(8,128)S(1)} %broadcast_select_fusion.32), channel_id=29, source_target_pairs={{0,1},{1,2},{2,3},{3,4},{4,5},{5,6},{6,7},{7,0},{8,9},{9,10},{10,1... | collective-permute-start | bytes 983048 | tf_op jit(solution)/vmap(transpose(jvp()))/dot_general | solution.py:9
  298.7 235.4 %collective-permute-start.28 = (f32[1,160,512]{2,1,0:T(8,128)}, f32[1,160,512]{2,1,0:T(8,128)}, u32[]{:S(2)}, u32[]{:S(2)}) collective-permute-start(f32[1,160,512]{2,1,0:T(8,128)} %get-tuple-element.45), channel_id=32, source_target_pairs={{0,1},{1,2},{2,3},{3,4},{4,5},{5,6},{6,7},{7,0},{8,9},{9,10},{10,1... | collective-permute-start | bytes 983048 | tf_op jit(solution)/vmap(transpose(jvp()))/dot_general | solution.py:9
  332.4 11.9 %collective-permute-start.12 = (f32[1,64,1280]{2,1,0:T(8,128)S(1)}, f32[1,64,1280]{2,1,0:T(8,128)S(1)}, u32[]{:S(2)}, u32[]{:S(2)}) collective-permute-start(f32[1,64,1280]{2,1,0:T(8,128)S(1)} %broadcast_select_fusion.30), channel_id=22, source_target_pairs={{0,1},{1,2},{2,3},{3,4},{4,5},{5,6},{6,7},{7,0},{8,9},{9,10},{10,1... | collective-permute-start | bytes 983048 | tf_op jit(solution)/vmap(transpose(jvp()))/dot_general | solution.py:21
  332.9 11.3 %collective-permute-start.13 = (f32[1,64,1280]{2,1,0:T(8,128)S(1)}, f32[1,64,1280]{2,1,0:T(8,128)S(1)}, u32[]{:S(2)}, u32[]{:S(2)}) collective-permute-start(f32[1,64,1280]{2,1,0:T(8,128)S(1)} %broadcast_select_fusion.31), channel_id=21, source_target_pairs={{0,7},{1,0},{2,1},{3,2},{4,3},{5,4},{6,5},{7,6},{8,15},{9,8},{10,9... | collective-permute-start | bytes 983048 | tf_op jit(solution)/vmap(transpose(jvp()))/dot_general | solution.py:21
  344.3 10.9 %collective-permute-start.14 = (f32[1,64,1280]{2,1,0:T(8,128)S(1)}, f32[1,64,1280]{2,1,0:T(8,128)S(1)}, u32[]{:S(2)}, u32[]{:S(2)}) collective-permute-start(f32[1,64,1280]{2,1,0:T(8,128)S(1)} %get-tuple-element.482), channel_id=24, source_target_pairs={{0,1},{1,2},{2,3},{3,4},{4,5},{5,6},{6,7},{7,0},{8,9},{9,10},{10,1... | collective-permute-start | bytes 983048 | tf_op jit(solution)/vmap(transpose(jvp()))/dot_general | solution.py:21
  344.5 10.8 %collective-permute-start.15 = (f32[1,64,1280]{2,1,0:T(8,128)S(1)}, f32[1,64,1280]{2,1,0:T(8,128)S(1)}, u32[]{:S(2)}, u32[]{:S(2)}) collective-permute-start(f32[1,64,1280]{2,1,0:T(8,128)S(1)} %get-tuple-element.483), channel_id=23, source_target_pairs={{0,7},{1,0},{2,1},{3,2},{4,3},{5,4},{6,5},{7,6},{8,15},{9,8},{10,9... | collective-permute-start | bytes 983048 | tf_op jit(solution)/vmap(transpose(jvp()))/dot_general | solution.py:21
  357.0 12.0 %collective-permute-start.12 = (f32[1,64,1280]{2,1,0:T(8,128)S(1)}, f32[1,64,1280]{2,1,0:T(8,128)S(1)}, u32[]{:S(2)}, u32[]{:S(2)}) collective-permute-start(f32[1,64,1280]{2,1,0:T(8,128)S(1)} %broadcast_select_fusion.30), channel_id=22, source_target_pairs={{0,1},{1,2},{2,3},{3,4},{4,5},{5,6},{6,7},{7,0},{8,9},{9,10},{10,1... | collective-permute-start | bytes 983048 | tf_op jit(solution)/vmap(transpose(jvp()))/dot_general | solution.py:21
  369.2 11.9 %collective-permute-start.14 = (f32[1,64,1280]{2,1,0:T(8,128)S(1)}, f32[1,64,1280]{2,1,0:T(8,128)S(1)}, u32[]{:S(2)}, u32[]{:S(2)}) collective-permute-start(f32[1,64,1280]{2,1,0:T(8,128)S(1)} %get-tuple-element.482), channel_id=24, source_target_pairs={{0,1},{1,2},{2,3},{3,4},{4,5},{5,6},{6,7},{7,0},{8,9},{9,10},{10,1... | collective-permute-start | bytes 983048 | tf_op jit(solution)/vmap(transpose(jvp()))/dot_general | solution.py:21
  370.1 11.0 %collective-permute-start.15 = (f32[1,64,1280]{2,1,0:T(8,128)S(1)}, f32[1,64,1280]{2,1,0:T(8,128)S(1)}, u32[]{:S(2)}, u32[]{:S(2)}) collective-permute-start(f32[1,64,1280]{2,1,0:T(8,128)S(1)} %get-tuple-element.483), channel_id=23, source_target_pairs={{0,7},{1,0},{2,1},{3,2},{4,3},{5,4},{6,5},{7,6},{8,15},{9,8},{10,9... | collective-permute-start | bytes 983048 | tf_op jit(solution)/vmap(transpose(jvp()))/dot_general | solution.py:21
  381.9 154.1 %collective-permute-start.27 = (f32[1,64,1280]{2,1,0:T(8,128)}, f32[1,64,1280]{2,1,0:T(8,128)}, u32[]{:S(2)}, u32[]{:S(2)}) collective-permute-start(f32[1,64,1280]{2,1,0:T(8,128)} %get-tuple-element.43), channel_id=25, source_target_pairs={{0,1},{1,2},{2,3},{3,4},{4,5},{5,6},{6,7},{7,0},{8,9},{9,10},{10,1... | collective-permute-start | bytes 983048 | tf_op jit(solution)/vmap(transpose(jvp()))/dot_general | solution.py:21
  383.0 14.2 %collective-permute-start.8 = (f32[1,64,1280]{2,1,0:T(8,128)S(1)}, f32[1,64,1280]{2,1,0:T(8,128)S(1)}, u32[]{:S(2)}, u32[]{:S(2)}) collective-permute-start(f32[1,64,1280]{2,1,0:T(8,128)S(1)} %broadcast_select_fusion.28), channel_id=16, source_target_pairs={{0,1},{1,2},{2,3},{3,4},{4,5},{5,6},{6,7},{7,0},{8,9},{9,10},{10,1... | collective-permute-start | bytes 983048 | tf_op jit(solution)/vmap(transpose(jvp()))/dot_general | solution.py:21
  385.2 11.9 %collective-permute-start.9 = (f32[1,64,1280]{2,1,0:T(8,128)S(1)}, f32[1,64,1280]{2,1,0:T(8,128)S(1)}, u32[]{:S(2)}, u32[]{:S(2)}) collective-permute-start(f32[1,64,1280]{2,1,0:T(8,128)S(1)} %broadcast_select_fusion.29), channel_id=15, source_target_pairs={{0,7},{1,0},{2,1},{3,2},{4,3},{5,4},{6,5},{7,6},{8,15},{9,8},{10,9... | collective-permute-start | bytes 983048 | tf_op jit(solution)/vmap(transpose(jvp()))/dot_general | solution.py:21
  408.2 11.9 %collective-permute-start.8 = (f32[1,64,1280]{2,1,0:T(8,128)S(1)}, f32[1,64,1280]{2,1,0:T(8,128)S(1)}, u32[]{:S(2)}, u32[]{:S(2)}) collective-permute-start(f32[1,64,1280]{2,1,0:T(8,128)S(1)} %broadcast_select_fusion.28), channel_id=16, source_target_pairs={{0,1},{1,2},{2,3},{3,4},{4,5},{5,6},{6,7},{7,0},{8,9},{9,10},{10,1... | collective-permute-start | bytes 983048 | tf_op jit(solution)/vmap(transpose(jvp()))/dot_general | solution.py:21
  409.2 10.9 %collective-permute-start.9 = (f32[1,64,1280]{2,1,0:T(8,128)S(1)}, f32[1,64,1280]{2,1,0:T(8,128)S(1)}, u32[]{:S(2)}, u32[]{:S(2)}) collective-permute-start(f32[1,64,1280]{2,1,0:T(8,128)S(1)} %broadcast_select_fusion.29), channel_id=15, source_target_pairs={{0,7},{1,0},{2,1},{3,2},{4,3},{5,4},{6,5},{7,6},{8,15},{9,8},{10,9... | collective-permute-start | bytes 983048 | tf_op jit(solution)/vmap(transpose(jvp()))/dot_general | solution.py:21
  432.7 11.9 %collective-permute-start.4 = (f32[1,64,1280]{2,1,0:T(8,128)S(1)}, f32[1,64,1280]{2,1,0:T(8,128)S(1)}, u32[]{:S(2)}, u32[]{:S(2)}) collective-permute-start(f32[1,64,1280]{2,1,0:T(8,128)S(1)} %broadcast_select_fusion.26), channel_id=9, source_target_pairs={{0,1},{1,2},{2,3},{3,4},{4,5},{5,6},{6,7},{7,0},{8,9},{9,10},{10,1... | collective-permute-start | bytes 983048 | tf_op jit(solution)/vmap(transpose(jvp()))/dot_general | solution.py:20
  433.8 10.8 %collective-permute-start.5 = (f32[1,64,1280]{2,1,0:T(8,128)S(1)}, f32[1,64,1280]{2,1,0:T(8,128)S(1)}, u32[]{:S(2)}, u32[]{:S(2)}) collective-permute-start(f32[1,64,1280]{2,1,0:T(8,128)S(1)} %broadcast_select_fusion.27), channel_id=8, source_target_pairs={{0,7},{1,0},{2,1},{3,2},{4,3},{5,4},{6,5},{7,6},{8,15},{9,8},{10,9... | collective-permute-start | bytes 983048 | tf_op jit(solution)/vmap(transpose(jvp()))/dot_general | solution.py:20
  455.0 11.9 %collective-permute-start.4 = (f32[1,64,1280]{2,1,0:T(8,128)S(1)}, f32[1,64,1280]{2,1,0:T(8,128)S(1)}, u32[]{:S(2)}, u32[]{:S(2)}) collective-permute-start(f32[1,64,1280]{2,1,0:T(8,128)S(1)} %broadcast_select_fusion.26), channel_id=9, source_target_pairs={{0,1},{1,2},{2,3},{3,4},{4,5},{5,6},{6,7},{7,0},{8,9},{9,10},{10,1... | collective-permute-start | bytes 983048 | tf_op jit(solution)/vmap(transpose(jvp()))/dot_general | solution.py:20
  455.1 11.7 %collective-permute-start.5 = (f32[1,64,1280]{2,1,0:T(8,128)S(1)}, f32[1,64,1280]{2,1,0:T(8,128)S(1)}, u32[]{:S(2)}, u32[]{:S(2)}) collective-permute-start(f32[1,64,1280]{2,1,0:T(8,128)S(1)} %broadcast_select_fusion.27), channel_id=8, source_target_pairs={{0,7},{1,0},{2,1},{3,2},{4,3},{5,4},{6,5},{7,6},{8,15},{9,8},{10,9... | collective-permute-start | bytes 983048 | tf_op jit(solution)/vmap(transpose(jvp()))/dot_general | solution.py:20
  478.2 11.8 %collective-permute-start = (f32[1,64,1280]{2,1,0:T(8,128)}, f32[1,64,1280]{2,1,0:T(8,128)}, u32[]{:S(2)}, u32[]{:S(2)}) collective-permute-start(f32[1,64,1280]{2,1,0:T(8,128)} %broadcast_select_fusion.24), channel_id=3, source_target_pairs={{0,1},{1,2},{2,3},{3,4},{4,5},{5,6},{6,7},{7,0},{8,9},{9,10},{10,1... | collective-permute-start | bytes 983048 | tf_op jit(solution)/vmap(transpose(jvp()))/dot_general | solution.py:20
  478.2 11.7 %collective-permute-start.1 = (f32[1,64,1280]{2,1,0:T(8,128)S(1)}, f32[1,64,1280]{2,1,0:T(8,128)S(1)}, u32[]{:S(2)}, u32[]{:S(2)}) collective-permute-start(f32[1,64,1280]{2,1,0:T(8,128)S(1)} %broadcast_select_fusion.25), channel_id=2, source_target_pairs={{0,7},{1,0},{2,1},{3,2},{4,3},{5,4},{6,5},{7,6},{8,15},{9,8},{10,9... | collective-permute-start | bytes 983048 | tf_op jit(solution)/vmap(transpose(jvp()))/dot_general | solution.py:20
  503.5 11.8 %collective-permute-start = (f32[1,64,1280]{2,1,0:T(8,128)}, f32[1,64,1280]{2,1,0:T(8,128)}, u32[]{:S(2)}, u32[]{:S(2)}) collective-permute-start(f32[1,64,1280]{2,1,0:T(8,128)} %broadcast_select_fusion.24), channel_id=3, source_target_pairs={{0,1},{1,2},{2,3},{3,4},{4,5},{5,6},{6,7},{7,0},{8,9},{9,10},{10,1... | collective-permute-start | bytes 983048 | tf_op jit(solution)/vmap(transpose(jvp()))/dot_general | solution.py:20
  503.5 11.7 %collective-permute-start.1 = (f32[1,64,1280]{2,1,0:T(8,128)S(1)}, f32[1,64,1280]{2,1,0:T(8,128)S(1)}, u32[]{:S(2)}, u32[]{:S(2)}) collective-permute-start(f32[1,64,1280]{2,1,0:T(8,128)S(1)} %broadcast_select_fusion.25), channel_id=2, source_target_pairs={{0,7},{1,0},{2,1},{3,2},{4,3},{5,4},{6,5},{7,6},{8,15},{9,8},{10,9... | collective-permute-start | bytes 983048 | tf_op jit(solution)/vmap(transpose(jvp()))/dot_general | solution.py:20
  517.0 11.8 %collective-permute-start.2 = (f32[1,64,1280]{2,1,0:T(8,128)}, f32[1,64,1280]{2,1,0:T(8,128)S(1)}, u32[]{:S(2)}, u32[]{:S(2)}) collective-permute-start(f32[1,64,1280]{2,1,0:T(8,128)} %get-tuple-element.455), channel_id=5, source_target_pairs={{0,1},{1,2},{2,3},{3,4},{4,5},{5,6},{6,7},{7,0},{8,9},{9,10},{10,1... | collective-permute-start | bytes 983048 | tf_op jit(solution)/vmap(transpose(jvp()))/dot_general | solution.py:20
  517.0 12.5 %collective-permute-start.3 = (f32[1,64,1280]{2,1,0:T(8,128)S(1)}, f32[1,64,1280]{2,1,0:T(8,128)}, u32[]{:S(2)}, u32[]{:S(2)}) collective-permute-start(f32[1,64,1280]{2,1,0:T(8,128)S(1)} %get-tuple-element.456), channel_id=4, source_target_pairs={{0,7},{1,0},{2,1},{3,2},{4,3},{5,4},{6,5},{7,6},{8,15},{9,8},{10,9... | collective-permute-start | bytes 983048 | tf_op jit(solution)/vmap(transpose(jvp()))/dot_general | solution.py:20
  532.2 14.1 %collective-permute-start.24 = (f32[1,64,1280]{2,1,0:T(8,128)S(1)}, f32[1,64,1280]{2,1,0:T(8,128)S(1)}, u32[]{:S(2)}, u32[]{:S(2)}) collective-permute-start(f32[1,64,1280]{2,1,0:T(8,128)S(1)} %get-tuple-element.37), channel_id=6, source_target_pairs={{0,1},{1,2},{2,3},{3,4},{4,5},{5,6},{6,7},{7,0},{8,9},{9,10},{10,1... | collective-permute-start | bytes 983048 | tf_op jit(solution)/vmap(transpose(jvp()))/dot_general | solution.py:20
  568.0 78.5 %all-gather.12.cloned.1.call-start = ((), (), s32[]{:S(2)}) async-start(), calls=%async_computation.1 | async-start | bytes 2949120 | tf_op jit(solution)/reshape | solution.py:58
  570.7 115.7 %all-gather.10.cloned.1.call-start = ((), (), s32[]{:S(2)}) async-start(), calls=%async_computation | async-start | bytes 2949120 | tf_op jit(solution)/reshape | solution.py:58
  (67 other events, 879.9 us)
Sparse Core Ops, SparseCore 0:
  568.2 38.4 all-gather.13
  608.8 37.6 all-gather.11
  648.7 37.6 all-gather.9
where the time goes:
time: 710 us; the launch traced here: 700 us
  matrix products  260 us (37%)
  waiting for transfers between devices  151 us (21%)
  starting transfers between devices  86.3 us (12%)
  local copies, waits for them, and re-layouts  75.8 us (11%)
  other arithmetic  68.9 us (10%)
  loops' own time  25 us (4%)
  between operations  17.6 us (2%)
  blocking collectives  15.3 us (2%)
    reshape x3, waiting for transfers between devices, step(): t.reshape(-1, *t.shape[2:])  113 us
    dot_general x11, matrix products, layer(): gate = jnp.dot(a, w['w_gate'], preferred_element_type=jnp.float32)  96.2 us
    dot_general x11, matrix products, layer(): up = jnp.dot(a, w['w_up'], preferred_element_type=jnp.float32)  87.5 us
    dot_general x11, matrix products, matmul(): jnp.dot(a, w, preferred_element_type=jnp.float32).astype(jnp.bfloat16)  76.4 us
    unnamed x57, local copies, waits for them, and re-layouts  66.6 us
    dot_general x18, starting transfers between devices, matmul(): jnp.dot(a, w, preferred_element_type=jnp.float32).astype(jnp.bfloat16)  31.3 us
    dot_general x18, starting transfers between devices, layer(): gate = jnp.dot(a, w['w_gate'], preferred_element_type=jnp.float32)  27.7 us
    dot_general x18, starting transfers between devices, layer(): up = jnp.dot(a, w['w_up'], preferred_element_type=jnp.float32)  27.1 us
  transfers between devices with their start and end apart: 57, of which 17 were waited for; matrix products, arithmetic and copies ran while one was open for 33% of the time, Pallas kernels for 0%

commit v1 on v0

v1 whole, which is shorter than its diff:
```python
import functools

import jax
import jax.numpy as jnp
from jax import lax
from jax.experimental import pallas as pl
from jax.experimental.pallas import tpu as pltpu
from jax.sharding import PartitionSpec as P

BF16, F32 = jnp.bfloat16, jnp.float32
FB = 256
TF = 512
TB = 1024


def dot(a, b):
    return jnp.dot(a, b, preferred_element_type=F32)


def dot_nt(a, b):
    return lax.dot_general(a, b, (((1,), (1,)), ((), ())), preferred_element_type=F32)


def scale_of(wide):
    return lax.rsqrt(jnp.mean(wide * wide, -1, keepdims=True) + 1e-6)


def sigmoid(g):
    return 0.5 * jnp.tanh(0.5 * g) + 0.5


def forward(x, dy, w, h, a2, a_t, dy_t, hid):
    wg, wu, wd = w
    blocks = wg.shape[2] // FB

    def tile(i, _):
        rows = pl.ds(pl.multiple_of(i * TF, TF), TF)
        wide = x[rows, :].astype(F32)
        a = (wide * scale_of(wide)).astype(BF16)
        for j in range(blocks):
            cols = pl.ds(j * FB, FB)
            gate, up = dot(a, wg[0, :, cols]), dot(a, wu[0, :, cols])
            hid[:, cols] = (gate * sigmoid(gate) * up).astype(BF16)
        out = dot(hid[...], wd[0]).astype(BF16).astype(F32)
        state = (wide + out).astype(BF16)
        h[rows, :] = state
        wide = state.astype(F32)
        n = (wide * scale_of(wide)).astype(BF16)
        a2[rows, :] = n
        a_t[:, rows] = n.T
        dy_t[:, rows] = dy[rows, :].T
        x[rows, :] = a
        return 0

    lax.fori_loop(0, x.shape[0] // TF, tile, 0)


def backward_tile(layer, j, i, a_ref, a_t, dy, dy_t, w, acc, da):
    wg, wu, wd = w
    rows = pl.ds(pl.multiple_of(i * TB, TB), TB)
    cols = pl.ds(pl.multiple_of(j * FB, FB), FB)
    acc_g, acc_u, acc_d = acc
    hids, dgates, dups = [], [], []
    half = TB // 2
    for s in range(2):
        sub = pl.ds(pl.multiple_of(i * TB + s * half, half), half)
        a = a_ref[sub, :]
        gate, up = dot(a, wg[layer, :, cols]), dot(a, wu[layer, :, cols])
        dh = dot_nt(dy[sub, :], wd[layer, cols, :]).astype(BF16).astype(F32)
        sg = sigmoid(gate)
        silu = gate * sg
        hids.append((silu * up).astype(BF16))
        dups.append((dh * silu).astype(BF16))
        dgates.append((dh * up * (sg + silu * (1.0 - sg))).astype(BF16))
        if da is not None:
            term = dot_nt(dgates[s], wg[layer, :, cols]) + dot_nt(dups[s], wu[layer, :, cols])

            @pl.when(j == 0)
            def _(sub=sub, term=term):
                da[sub, :] = term

            @pl.when(j > 0)
            def _(sub=sub, term=term):
                da[sub, :] += term

    hid, dgate, dup = (jnp.concatenate(t, 0) for t in (hids, dgates, dups))
    terms = dot(a_t[:, rows], dgate), dot(a_t[:, rows], dup), dot(dy_t[:, rows], hid)

    @pl.when(i == 0)
    def _():
        for to, term in zip(acc, terms, strict=True):
            to[...] = term

    @pl.when(i > 0)
    def _():
        for to, term in zip(acc, terms, strict=True):
            to[...] += term


def backward(layer, a_ref, a_t, dy, dy_t, w, acc, da, grads):
    steps = dy.shape[0] // TB
    gg, gu, gd = grads

    def block(j, _):
        def tile(i, _):
            backward_tile(layer, j, i, a_ref, a_t, dy, dy_t, w, acc, da)
            return 0

        lax.fori_loop(0, steps, tile, 0)
        cols = pl.ds(pl.multiple_of(j * FB, FB), FB)
        gg[layer, :, cols] = acc[0][...].astype(BF16)
        gu[layer, :, cols] = acc[1][...].astype(BF16)
        gd[layer, cols, :] = acc[2][...].astype(BF16).T
        return 0

    lax.fori_loop(0, w[0].shape[2] // FB, block, 0)


def between(a1, h, dy, a_t, dy_t, da):
    def tile(i, _):
        rows = pl.ds(pl.multiple_of(i * TF, TF), TF)
        wide = h[rows, :].astype(F32)
        by_a = da[rows, :].astype(BF16).astype(F32)
        scale = scale_of(wide)
        inner = jnp.mean(by_a * wide, -1, keepdims=True)
        by_h = scale * by_a - wide * (scale * scale * scale * inner)
        total = (dy[rows, :].astype(F32) + by_h.astype(BF16).astype(F32)).astype(BF16)
        dy[rows, :] = total
        dy_t[:, rows] = total.T
        a_t[:, rows] = a1[rows, :].T
        return 0

    lax.fori_loop(0, h.shape[0] // TF, tile, 0)


def kernel(x_in, dy_in, wg_in, wu_in, wd_in, gg, gu, gd, x, dy, wg, wu, wd, h, a2, a_t, dy_t, hid, da, ag, au, ad, sems):
    copies = [
        pltpu.make_async_copy(src, dst, sems.at[k])
        for k, (src, dst) in enumerate(((x_in.at[0], x), (dy_in.at[0], dy), (wg_in, wg), (wu_in, wu), (wd_in, wd)))
    ]
    for c in copies:
        c.start()
    for c in copies:
        c.wait()
    w, acc, grads = (wg, wu, wd), (ag, au, ad), (gg, gu, gd)
    forward(x, dy, w, h, a2, a_t, dy_t, hid)
    backward(1, a2, a_t, dy, dy_t, w, acc, da, grads)
    between(x, h, dy, a_t, dy_t, da)
    backward(0, x, a_t, dy, dy_t, w, acc, None, grads)


def gradients(x, dy, wg, wu, wd):
    _, t, d = x.shape
    ff = wg.shape[2]
    any_, vm = pl.BlockSpec(memory_space=pl.ANY), pl.BlockSpec(memory_space=pltpu.VMEM)
    return pl.pallas_call(
        kernel,
        out_shape=[jax.ShapeDtypeStruct(w.shape, BF16) for w in (wg, wu, wd)],
        in_specs=[any_] * 5,
        out_specs=[vm] * 3,
        scratch_shapes=[
            pltpu.VMEM((t, d), BF16),
            pltpu.VMEM((t, d), BF16),
            pltpu.VMEM(wg.shape, BF16),
            pltpu.VMEM(wu.shape, BF16),
            pltpu.VMEM(wd.shape, BF16),
            pltpu.VMEM((t, d), BF16),
            pltpu.VMEM((t, d), BF16),
            pltpu.VMEM((d, t), BF16),
            pltpu.VMEM((d, t), BF16),
            pltpu.VMEM((TF, ff), BF16),
            pltpu.VMEM((t, d), F32),
            pltpu.VMEM((d, FB), F32),
            pltpu.VMEM((d, FB), F32),
            pltpu.VMEM((d, FB), F32),
            pltpu.SemaphoreType.DMA((5,)),
        ],
        compiler_params=pltpu.CompilerParams(vmem_limit_bytes=67_000_000),
        name="gradients",
    )(x, dy, wg, wu, wd)


def solution(mesh):
    def step(x, dy, *arrays):
        weights, m, v = (arrays[i : i + 3] for i in (0, 3, 6))
        n = lax.axis_size("dp")
        me = lax.axis_index("dp")
        terms = gradients(x, dy, *weights)
        g = [lax.psum_scatter(t, "dp", scatter_dimension=1, tiled=True).astype(F32) for t in terms]
        count = sum(w.size for w in weights)
        squares = lax.psum(sum(jnp.sum(t * t) for t in g), "dp")
        factor = jnp.minimum(1.0, 0.5 * lax.rsqrt(squares / count + 1e-30))
        new = ([], [], [])
        for w, m_, v_, t in zip(weights, m, v, g, strict=True):
            t = t * factor
            rows = w.shape[1] // n
            own = lax.dynamic_slice_in_dim(w, me * rows, rows, 1).astype(F32)
            m_ = 0.9 * m_ + 0.1 * t
            v_ = 0.95 * v_ + 0.05 * t * t
            own = (own - 0.02 * (m_ * lax.rsqrt(v_ + 1e-8) + 0.1 * own)).astype(BF16)
            new[0].append(lax.all_gather(own, "dp", axis=1, tiled=True))
            new[1].append(m_)
            new[2].append(v_)
        return tuple(t for three in new for t in three)

    seq, whole, block = P(("rep", "dp"), None, None), P(None, None, None), P(None, "dp", None)
    return jax.shard_map(
        step,
        mesh=mesh,
        in_specs=(seq, seq, *[whole] * 3, *[block] * 6),
        out_specs=(*[P("rep", None, None)] * 3, *[P("rep", "dp", None)] * 6),
        check_vma=False,
    )
```

time: 710 us -> 455 us (0.64); the launches traced: 700 us -> 455 us
  matrix products: 260 us -> 0 us
  Pallas kernels: 0 us -> 162 us
  waiting for transfers between devices: 151 us -> 239 us
  starting transfers between devices: 86.3 us -> 0.38 us
  local copies, waits for them, and re-layouts: 75.8 us -> 7.77 us
  other arithmetic: 68.9 us -> 12.7 us
  loops' own time: 25 us -> 0 us
    dot_general x33 -> x0, matrix products: 260 us -> none  [the longest x11 96.2 us: layer(): gate = jnp.dot(a, w['w_gate'], preferred_element_type=jnp.float32)]
    pallas_call x0 -> x1, Pallas kernels: none -> 162 us  [gradients(): pl.pallas_call(kernel, out_shape=[jax.ShapeDtypeStruct(w.shape, BF16) for...]
    reduce_scatter x0 -> x3, waiting for transfers between devices: none -> 125 us  [step(): lax.psum_scatter(t, 'dp', scatter_dimension=1, tiled=True).astype(F32)]
    reshape x3 -> x0, waiting for transfers between devices: 113 us -> none  [step(): t.reshape(-1, *t.shape[2:])]
    all_gather x0 -> x3, waiting for transfers between devices: none -> 113 us  [step(): new[0].append(lax.all_gather(own, 'dp', axis=1, tiled=True))]
    dot_general x54 -> x0, starting transfers between devices: 86.1 us -> none  [the longest x18 31.3 us: matmul(): jnp.dot(a, w, preferred_element_type=jnp.float32).astype(jnp.bfloat16)]
    unnamed x57 -> x21, local copies, waits for them, and re-layouts: 66.6 us -> 7.77 us
    dot_general x54 -> x0, waiting for transfers between devices: 37.8 us -> none  [the longest x18 18.9 us: matmul(): jnp.dot(a, w, preferred_element_type=jnp.float32).astype(jnp.bfloat16)]
  transfers between devices with their start and end apart: 57 -> 6, of which waited for: 17 -> 6; matrix products, arithmetic and copies ran while one was open for 33% -> 2% of each run, Pallas kernels for 0% -> 0%
where the time goes in v1:
time: 455 us
  waiting for transfers between devices  239 us (53%)
  Pallas kernels  162 us (36%)
  between operations  16.9 us (4%)
  blocking collectives  16.1 us (4%)
  other arithmetic  12.7 us (3%)
  local copies, waits for them, and re-layouts  7.77 us (2%)
    pallas_call x1, Pallas kernels, gradients(): pl.pallas_call(kernel, out_shape=[jax.ShapeDtypeStruct(w.shape, BF16) for...  162 us
    reduce_scatter x3, waiting for transfers between devices, step(): lax.psum_scatter(t, 'dp', scatter_dimension=1, tiled=True).astype(F32)  125 us
    all_gather x3, waiting for transfers between devices, step(): new[0].append(lax.all_gather(own, 'dp', axis=1, tiled=True))  113 us
    psum x1, blocking collectives, step(): squares = lax.psum(sum((jnp.sum(t * t) for t in g)), 'dp')  16.1 us
  transfers between devices with their start and end apart: 6, of which 6 were waited for; matrix products, arithmetic and copies ran while one was open for 2% of the time, Pallas kernels for 0%

profile of v1, /device:TPU:22, one launch (start us, length us, event | category | flops | bytes accessed | tf_op | source)
XLA Modules:
  0.0 454.5 jit_solution(3009793050479264853)
XLA Ops:
  7.2 0.1 reduce-scatter.4.cloned.1.call-start
  7.3 161.8 %gradients.1 = (bf16[2,512,1280]{2,1,0:T(8,128)(2,1)}, bf16[2,512,1280]{2,1,0:T(8,128)(2,1)}, bf16[2,1280,512]{2,1,0:T(8,128)(2,1)}) custom-call(bf16[1,4096,512]{2,1,0:T(8,128)(2,1)} %x_in.1, bf16[1,4096,512]{2,1,0:T(8,128)(2,1)} %dy_in.1, bf16[2,512,1280]{2,1,0:T(8,128)(2,1)} %wg_in.1, bf16[2,512,1280]{2,1,0:T(8,128)(2,1)} %wu_in.1, ...), custom_call_target="tpu_custom_call" | custom-call | tf_op jit(solution)/shard_map/gradients/pallas_call | solution.py:156
  169.1 0.1 reduce-scatter.4.cloned.1.call-update
  169.1 0.1 reduce-scatter.6.cloned.1.call-start
  169.2 0.0 copy-start.4
  169.2 0.7 reduce-scatter.6.cloned.1.call-update
  169.9 0.1 reduce-scatter.8.cloned.1.call-start
  170.0 0.7 reduce-scatter.8.cloned.1.call-update
  170.7 0.0 copy-start.6
  170.8 0.1 all-gather.8.cloned.1.call-start
  170.8 43.2 %reduce-scatter.4.cloned.1.call-done = bf16[2,64,1280]{2,1,0:T(8,128)(2,1)} async-done(((bf16[2,512,1280]{2,1,0:T(8,128)(2,1)}), bf16[2,64,1280]{2,1,0:T(8,128)(2,1)}) %reduce-scatter.4.cloned.1.call-update) | async-done | bytes 327696 | tf_op jit(solution)/shard_map/reduce_scatter | solution.py:189
  214.1 1.8 fusion.9
  215.9 41.4 %reduce-scatter.6.cloned.1.call-done = bf16[2,64,1280]{2,1,0:T(8,128)(2,1)} async-done(((bf16[2,512,1280]{2,1,0:T(8,128)(2,1)}), bf16[2,64,1280]{2,1,0:T(8,128)(2,1)}) %reduce-scatter.6.cloned.1.call-update) | async-done | bytes 327696 | tf_op jit(solution)/shard_map/reduce_scatter | solution.py:189
  257.3 1.7 fusion.10
  260.3 40.1 %reduce-scatter.8.cloned.1.call-done = bf16[2,160,512]{2,1,0:T(8,128)(2,1)} async-done(((bf16[2,1280,512]{2,1,0:T(8,128)(2,1)}), bf16[2,160,512]{2,1,0:T(8,128)(2,1)}) %reduce-scatter.8.cloned.1.call-update) | async-done | bytes 327696 | tf_op jit(solution)/shard_map/reduce_scatter | solution.py:189
  300.4 1.7 fusion.11
  302.8 16.1 %psum.7 = f32[]{:T(128)} all-reduce(f32[]{:T(128)S(6)} %add.65), channel_id=1, replica_groups=mesh['rep'=8,'dp'=8] {'dp'}, use_global_device_ids=true, to_apply=%region_6.0 | all-reduce | flops 1 | bytes 8 | tf_op jit(solution)/shard_map/psum | solution.py:191
  319.6 2.4 fusion.17
  322.1 0.1 all-gather.8.cloned.1.call-update
  322.1 0.1 all-gather.4.cloned.1.call-start
  322.2 2.4 fusion.8
  324.6 0.1 all-gather.4.cloned.1.call-update
  324.7 0.1 all-gather.6.cloned.1.call-start
  324.8 2.5 fusion.14
  327.3 0.1 all-gather.6.cloned.1.call-update
  327.4 33.2 %all-gather.8.cloned.1.call-done = bf16[2,1280,512]{2,1,0:T(8,128)(2,1)} async-done(((bf16[2,160,512]{2,1,0:T(8,128)(2,1)}), bf16[2,1280,512]{2,1,0:T(8,128)(2,1)}) %all-gather.8.cloned.1.call-update) | async-done | bytes 2621456 | tf_op jit(solution)/shard_map/all_gather | solution.py:201
  360.5 39.7 %all-gather.4.cloned.1.call-done = bf16[2,512,1280]{2,1,0:T(8,128)(2,1)} async-done(((bf16[2,64,1280]{2,1,0:T(8,128)(2,1)}), bf16[2,512,1280]{2,1,0:T(8,128)(2,1)}) %all-gather.4.cloned.1.call-update) | async-done | bytes 2621456 | tf_op jit(solution)/shard_map/all_gather | solution.py:201
  400.2 39.7 %all-gather.6.cloned.1.call-done = bf16[2,512,1280]{2,1,0:T(8,128)(2,1)} async-done(((bf16[2,64,1280]{2,1,0:T(8,128)(2,1)}), bf16[2,512,1280]{2,1,0:T(8,128)(2,1)}) %all-gather.6.cloned.1.call-update) | async-done | bytes 2621456 | tf_op jit(solution)/shard_map/all_gather | solution.py:201
  440.0 3.5 copy.23
  443.5 1.5 copy.24
  445.0 1.2 copy-done
  446.2 1.5 copy.25
  (15 shorter events, 0.0 us)
Async XLA Ops:
  7.2 206.9 %reduce-scatter.4.cloned.1.call-start = ((), (), s32[]{:S(2)}) async-start(), calls=%async_computation.3 | async-start | bytes 2949120 | tf_op jit(solution)/shard_map/reduce_scatter | solution.py:189
  169.1 88.1 %reduce-scatter.6.cloned.1.call-start = ((), (), s32[]{:S(2)}) async-start(), calls=%async_computation.4 | async-start | bytes 2949120 | tf_op jit(solution)/shard_map/reduce_scatter | solution.py:189
  169.2 150.4 %copy-start.4 = (f32[2,160,512]{2,1,0:T(8,128)S(1)}, f32[2,160,512]{2,1,0:T(8,128)}, u32[]{:S(2)}) copy-start(f32[2,160,512]{2,1,0:T(8,128)} %param.21) | copy-start | bytes 1966084
  169.2 150.4 %copy-start.5 = (f32[2,160,512]{2,1,0:T(8,128)S(1)}, f32[2,160,512]{2,1,0:T(8,128)}, u32[]{:S(2)}) copy-start(f32[2,160,512]{2,1,0:T(8,128)} %param.18) | copy-start | bytes 1966084
  169.9 130.4 %reduce-scatter.8.cloned.1.call-start = ((), (), s32[]{:S(2)}) async-start(), calls=%async_computation.5 | async-start | bytes 2949120 | tf_op jit(solution)/shard_map/reduce_scatter | solution.py:189
  170.7 151.5 %copy-start.6 = (f32[2,64,1280]{2,1,0:T(8,128)S(1)}, f32[2,64,1280]{2,1,0:T(8,128)}, u32[]{:S(2)}) copy-start(f32[2,64,1280]{2,1,0:T(8,128)} %param.19) | copy-start | bytes 1966084
  170.7 151.5 %copy-start.7 = (f32[2,64,1280]{2,1,0:T(8,128)S(1)}, f32[2,64,1280]{2,1,0:T(8,128)}, u32[]{:S(2)}) copy-start(f32[2,64,1280]{2,1,0:T(8,128)} %param.16) | copy-start | bytes 1966084
  170.8 189.8 %all-gather.8.cloned.1.call-start = ((), (), s32[]{:S(2)}) async-start(), calls=%async_computation.8 | async-start | bytes 2949120 | tf_op jit(solution)/shard_map/all_gather | solution.py:201
  214.1 108.2 %copy-start.3 = (bf16[2,64,1280]{2,1,0:T(8,128)(2,1)S(1)}, bf16[2,64,1280]{2,1,0:T(8,128)(2,1)}, u32[]{:S(2)}) copy-start(bf16[2,64,1280]{2,1,0:T(8,128)(2,1)} %reduce-scatter.4.cloned.1.call-done) | copy-start | bytes 983044
  322.1 2.7 copy-start.2
  322.1 2.7 copy-start.8
  322.1 78.1 %all-gather.4.cloned.1.call-start = ((), (), s32[]{:S(2)}) async-start(), calls=%async_computation.6 | async-start | bytes 2949120 | tf_op jit(solution)/shard_map/all_gather | solution.py:201
  324.7 115.3 %all-gather.6.cloned.1.call-start = ((), (), s32[]{:S(2)}) async-start(), calls=%async_computation.7 | async-start | bytes 2949120 | tf_op jit(solution)/shard_map/all_gather | solution.py:201
  439.9 3.6 copy-start.1
  443.5 2.7 copy-start
Sparse Core Ops, SparseCore 0:
  169.2 44.7 reduce-scatter.3
  217.0 40.2 reduce-scatter.5
  260.2 40.1 reduce-scatter.7
  322.3 38.2 all-gather.7
  362.6 37.6 all-gather.3
  402.3 37.6 all-gather.5

commit v2 on v1

--- a/solution.py
+++ b/solution.py
@@ -97,25 +97,6 @@
             to[...] += term
 
 
-def backward(layer, a_ref, a_t, dy, dy_t, w, acc, da, grads):
-    steps = dy.shape[0] // TB
-    gg, gu, gd = grads
-
-    def block(j, _):
-        def tile(i, _):
-            backward_tile(layer, j, i, a_ref, a_t, dy, dy_t, w, acc, da)
-            return 0
-
-        lax.fori_loop(0, steps, tile, 0)
-        cols = pl.ds(pl.multiple_of(j * FB, FB), FB)
-        gg[layer, :, cols] = acc[0][...].astype(BF16)
-        gu[layer, :, cols] = acc[1][...].astype(BF16)
-        gd[layer, cols, :] = acc[2][...].astype(BF16).T
-        return 0
-
-    lax.fori_loop(0, w[0].shape[2] // FB, block, 0)
-
-
 def between(a1, h, dy, a_t, dy_t, da):
     def tile(i, _):
         rows = pl.ds(pl.multiple_of(i * TF, TF), TF)
@@ -133,79 +114,300 @@
     lax.fori_loop(0, h.shape[0] // TF, tile, 0)
 
 
-def kernel(x_in, dy_in, wg_in, wu_in, wd_in, gg, gu, gd, x, dy, wg, wu, wd, h, a2, a_t, dy_t, hid, da, ag, au, ad, sems):
+def exchanged(me, n):
+    return lax.rem(me + 1, n), lax.rem(me + n - 1, n)
+
+
+def remote(src, dst, send, recv, to):
+    return pltpu.make_async_remote_copy(
+        src_ref=src, dst_ref=dst, send_sem=send, recv_sem=recv, device_id={"dp": to}, device_id_type=pl.DeviceIdType.MESH
+    )
+
+
+class Ring:
+    def __init__(self, terms, slots, send, recv, rows, me, n):
+        self.terms, self.slots, self.send, self.recv, self.rows, self.me, self.n = terms, slots, send, recv, rows, me, n
+
+    def chunk(self, way, hop):
+        at = lax.rem(self.me + self.n - 1 - hop, self.n) if way == 0 else lax.rem(self.me + 1 + hop, self.n)
+        return pl.ds(pl.multiple_of(at * self.rows[0], self.rows[2]) + self.rows[1], self.rows[2])
+
+    def copy(self, way, hop):
+        return remote(
+            self.terms[way].at[self.chunk(way, hop), :],
+            self.slots[way].at[hop],
+            self.send.at[way, hop],
+            self.recv.at[way, hop],
+            exchanged(self.me, self.n)[way],
+        )
+
+    def begin(self):
+        for way in range(2):
+            self.copy(way, 0).start()
+
+    def add(self, hop):
+        for way in range(2):
+            self.copy(way, hop - 1).wait()
+        for way in range(2):
+            at = self.chunk(way, hop)
+            own = self.terms[way][at, :].astype(F32)
+            self.terms[way][at, :] = (own + self.slots[way][hop - 1].astype(F32)).astype(BF16)
+
+    def go_on(self, hop):
+        for way in range(2):
+            self.copy(way, hop).start()
+
+
+def kernel(n, x_in, dy_in, wg_in, wu_in, wd_in, mg_in, mu_in, md_in, vg_in, vu_in, vd_in,
+           og, ou, od, mg_out, mu_out, md_out, vg_out, vu_out, vd_out,
+           x, dy, wg, wu, wd, h, a2, a_t, dy_t, hid, da, ag, au, ad,
+           tg, tu, td, slot_g, slot_u, slot_d, mg, mu, md, vg, vu, vd, ng, nu, nd, mine, others,
+           sems, msems, rs_send, rs_recv, rd_send, rd_recv, sq_send, sq_recv, ag_send, ag_recv, osems):
+    me = lax.axis_index("dp")
+    layers, d, ff = wg.shape
+    blocks = ff // FB
+    ticks = n // 2
+    pieces = layers * blocks
     copies = [
         pltpu.make_async_copy(src, dst, sems.at[k])
         for k, (src, dst) in enumerate(((x_in.at[0], x), (dy_in.at[0], dy), (wg_in, wg), (wu_in, wu), (wd_in, wd)))
     ]
-    for c in copies:
+    moments = (mg, mu, md, vg, vu, vd)
+    later = [
+        pltpu.make_async_copy(src, dst, msems.at[k])
+        for k, (src, dst) in enumerate(zip((mg_in, mu_in, md_in, vg_in, vu_in, vd_in), moments, strict=True))
+    ]
+    for c in copies + later:
         c.start()
+    barrier = pltpu.get_barrier_semaphore()
+    for off in range(1, n):
+        pl.semaphore_signal(barrier, 1, device_id={"dp": lax.rem(me + off, n)}, device_id_type=pl.DeviceIdType.MESH)
+    pl.semaphore_wait(barrier, n - 1)
     for c in copies:
         c.wait()
-    w, acc, grads = (wg, wu, wd), (ag, au, ad), (gg, gu, gd)
+    w, acc = (wg, wu, wd), (ag, au, ad)
     forward(x, dy, w, h, a2, a_t, dy_t, hid)
-    backward(1, a2, a_t, dy, dy_t, w, acc, da, grads)
+
+    per, per_d = d // n, ff // n
+    half = per_d // 2
+
+    def ring(p):
+        s = lax.rem(p, 3)
+        return Ring((tg.at[p], tu.at[p]), (slot_g.at[s], slot_u.at[s]), rs_send.at[s], rs_recv.at[s], (per, 0, per), me, n)
+
+    def ring_d(layer, part):
+        k = layer * 2 + part
+        terms = tuple(td.at[layer, way] for way in range(2))
+        slots = tuple(slot_d.at[k, way] for way in range(2))
+        return Ring(terms, slots, rd_send.at[k], rd_recv.at[k], (per_d, part * half, half), me, n)
+
+    def tick(p, i):
+        @pl.when(jnp.logical_and(p >= 2, p < pieces + 2))
+        def _():
+            old = ring(p - 2)
+            old.add(i + ticks)
+
+            @pl.when(i < ticks - 1)
+            def _():
+                old.go_on(i + ticks)
+
+        @pl.when(jnp.logical_and(p >= 1, p < pieces + 1))
+        def _():
+            new = ring(p - 1)
+
+            @pl.when(i > 0)
+            def _():
+                new.add(i)
+
+            new.go_on(i)
+
+    def tick_d(layer, step):
+        @pl.when(step == 0)
+        def _():
+            for part in range(2):
+                ring_d(layer, part).begin()
+
+        @pl.when(jnp.logical_and(step > 0, step < n))
+        def _():
+            for part in range(2):
+                one = ring_d(layer, part)
+                one.add(step)
+
+                @pl.when(step < n - 1)
+                def _(one=one):
+                    one.go_on(step)
+
+    def backward(layer, first, a_ref, da):
+        def block(j, _):
+            p = first + j
+
+            def tile(i, _):
+                tick(p, i)
+                if first:
+                    k = j * ticks + i
+
+                    @pl.when(lax.rem(k, 2) == 0)
+                    def _():
+                        tick_d(1, k // 2)
+
+                backward_tile(layer, j, i, a_ref, a_t, dy, dy_t, w, acc, da)
+                return 0
+
+            lax.fori_loop(0, ticks, tile, 0)
+            tg[p] = ag[...].astype(BF16)
+            tu[p] = au[...].astype(BF16)
+            rows = pl.ds(pl.multiple_of(j * FB, FB), FB)
+            by_down = ad[...].astype(BF16).T
+            td[layer, 0, rows, :] = by_down[:, : d // 2]
+            td[layer, 1, rows, :] = by_down[:, d // 2 :]
+            return 0
+
+        lax.fori_loop(0, blocks, block, 0)
+
+    backward(1, 0, a2, da)
     between(x, h, dy, a_t, dy_t, da)
-    backward(0, x, a_t, dy, dy_t, w, acc, None, grads)
-
-
-def gradients(x, dy, wg, wu, wd):
+    backward(0, blocks, x, None)
+
+    def drain(k, _):
+        tick(pieces + k // ticks, lax.rem(k, ticks))
+        tick_d(0, k)
+        return 0
+
+    lax.fori_loop(0, n, drain, 0)
+
+    own, own_d = pl.ds(pl.multiple_of(me * per, per), per), pl.ds(pl.multiple_of(me * per_d, per_d), per_d)
+    total = jnp.zeros((8, 128), F32)
+
+    def squares(t):
+        t = t.astype(F32)
+        return jnp.sum(t * t)
+
+    local = jnp.float32(0)
+    for p in range(pieces):
+        local += squares(tg[p, own, :]) + squares(tu[p, own, :])
+    for layer in range(layers):
+        for way in range(2):
+            local += squares(td[layer, way, own_d, :])
+    mine[...] = total + local
+    sent = [remote(mine, others.at[k - 1], sq_send.at[k - 1], sq_recv.at[k - 1], lax.rem(me + k, n)) for k in range(1, n)]
+    for c in sent:
+        c.start()
+    for c in later:
+        c.wait()
+    for c in sent:
+        c.wait()
+    summed = mine[...]
+    for k in range(n - 1):
+        summed = summed + others[k]
+    count = layers * d * ff * 3
+    factor = jnp.minimum(1.0, 0.5 * lax.rsqrt(summed[0:1, 0:1] / count + 1e-30))
+
+    def adamw(w_own, m_at, v_at, g, new):
+        g = g.astype(F32) * factor
+        m_ = 0.9 * m_at[...] + 0.1 * g
+        v_ = 0.95 * v_at[...] + 0.05 * g * g
+        m_at[...] = m_
+        v_at[...] = v_
+        w_own = w_own.astype(F32)
+        new[...] = (w_own - 0.02 * (m_ * lax.rsqrt(v_ + 1e-8) + 0.1 * w_own)).astype(BF16)
+
+    outs, news, owns = (og, ou, od), (ng, nu, nd), (own, own, own_d)
+
+    def gather(kind, way, hop):
+        layer = way
+        at = lax.rem(me + n - hop, n) if way == 0 else lax.rem(me + hop, n)
+        size = per_d if kind == 2 else per
+        rows = outs[kind].at[layer, pl.ds(pl.multiple_of(at * size, size), size), :]
+        src = news[kind].at[layer] if isinstance(hop, int) and hop == 0 else rows
+        return remote(src, rows, ag_send.at[way, hop, kind], ag_recv.at[way, hop, kind], exchanged(me, n)[way])
+
+    finals = []
+    for kind in range(3):
+        for layer in range(layers):
+            if kind < 2:
+                for j in range(blocks):
+                    cols = pl.ds(j * FB, FB)
+                    adamw(
+                        w[kind][layer, own, cols],
+                        (mg, mu)[kind].at[layer, :, cols],
+                        (vg, vu)[kind].at[layer, :, cols],
+                        (tg, tu)[kind][(layers - 1 - layer) * blocks + j, own, :],
+                        news[kind].at[layer, :, cols],
+                    )
+            else:
+                for way in range(2):
+                    cols = pl.ds(way * (d // 2), d // 2)
+                    adamw(wd[layer, own_d, cols], md.at[layer, :, cols], vd.at[layer, :, cols], td[layer, way, own_d, :], nd.at[layer, :, cols])
+            gather(kind, layer, 0).start()
+        finals.append(pltpu.make_async_copy(news[kind], outs[kind].at[:, owns[kind], :], osems.at[kind]))
+        finals.append(pltpu.make_async_copy(moments[kind], (mg_out, mu_out, md_out)[kind], osems.at[3 + kind]))
+        finals.append(pltpu.make_async_copy(moments[3 + kind], (vg_out, vu_out, vd_out)[kind], osems.at[6 + kind]))
+        for c in finals[-3:]:
+            c.start()
+    for hop in range(1, n):
+        for kind in range(3):
+            for way in range(2):
+                gather(kind, way, hop - 1).wait()
+                if hop < n - 1:
+                    gather(kind, way, hop).start()
+    for c in finals:
+        c.wait()
+
+
+def stepped(n, x, dy, *arrays):
     _, t, d = x.shape
-    ff = wg.shape[2]
-    any_, vm = pl.BlockSpec(memory_space=pl.ANY), pl.BlockSpec(memory_space=pltpu.VMEM)
+    wg, _, wd = arrays[:3]
+    layers, _, ff = wg.shape
+    per, per_d = d // n, ff // n
+    pieces = layers * (ff // FB)
+    any_ = pl.BlockSpec(memory_space=pl.ANY)
+    dma = pltpu.SemaphoreType.DMA
     return pl.pallas_call(
-        kernel,
-        out_shape=[jax.ShapeDtypeStruct(w.shape, BF16) for w in (wg, wu, wd)],
-        in_specs=[any_] * 5,
-        out_specs=[vm] * 3,
+        functools.partial(kernel, n),
+        out_shape=[jax.ShapeDtypeStruct(a.shape, a.dtype) for a in arrays],
+        in_specs=[any_] * 11,
+        out_specs=[any_] * 9,
         scratch_shapes=[
             pltpu.VMEM((t, d), BF16),
             pltpu.VMEM((t, d), BF16),
-            pltpu.VMEM(wg.shape, BF16),
-            pltpu.VMEM(wu.shape, BF16),
-            pltpu.VMEM(wd.shape, BF16),
+            *[pltpu.VMEM(w.shape, BF16) for w in arrays[:3]],
             pltpu.VMEM((t, d), BF16),
             pltpu.VMEM((t, d), BF16),
             pltpu.VMEM((d, t), BF16),
             pltpu.VMEM((d, t), BF16),
             pltpu.VMEM((TF, ff), BF16),
             pltpu.VMEM((t, d), F32),
-            pltpu.VMEM((d, FB), F32),
-            pltpu.VMEM((d, FB), F32),
-            pltpu.VMEM((d, FB), F32),
-            pltpu.SemaphoreType.DMA((5,)),
+            *[pltpu.VMEM((d, FB), F32)] * 3,
+            *[pltpu.VMEM((pieces, d, FB), BF16)] * 2,
+            pltpu.VMEM((layers, 2, ff, d // 2), BF16),
+            *[pltpu.VMEM((3, n - 1, per, FB), BF16)] * 2,
+            pltpu.VMEM((layers * 2, 2, n - 1, per_d // 2, d // 2), BF16),
+            *[pltpu.VMEM(a.shape, F32) for a in arrays[3:]],
+            *[pltpu.VMEM(a.shape, BF16) for a in arrays[3:6]],
+            pltpu.VMEM((8, 128), F32),
+            pltpu.VMEM((n - 1, 8, 128), F32),
+            dma((5,)),
+            dma((6,)),
+            dma((3, 2, n - 1)),
+            dma((3, 2, n - 1)),
+            dma((layers * 2, 2, n - 1)),
+            dma((layers * 2, 2, n - 1)),
+            dma((n - 1,)),
+            dma((n - 1,)),
+            dma((2, n - 1, 3)),
+            dma((2, n - 1, 3)),
+            dma((9,)),
         ],
-        compiler_params=pltpu.CompilerParams(vmem_limit_bytes=67_000_000),
-        name="gradients",
-    )(x, dy, wg, wu, wd)
+        compiler_params=pltpu.CompilerParams(vmem_limit_bytes=67_043_328, collective_id=0, has_side_effects=True),
+        name="step",
+    )(x, dy, *arrays)
 
 
 def solution(mesh):
-    def step(x, dy, *arrays):
-        weights, m, v = (arrays[i : i + 3] for i in (0, 3, 6))
-        n = lax.axis_size("dp")
-        me = lax.axis_index("dp")
-        terms = gradients(x, dy, *weights)
-        g = [lax.psum_scatter(t, "dp", scatter_dimension=1, tiled=True).astype(F32) for t in terms]
-        count = sum(w.size for w in weights)
-        squares = lax.psum(sum(jnp.sum(t * t) for t in g), "dp")
-        factor = jnp.minimum(1.0, 0.5 * lax.rsqrt(squares / count + 1e-30))
-        new = ([], [], [])
-        for w, m_, v_, t in zip(weights, m, v, g, strict=True):
-            t = t * factor
-            rows = w.shape[1] // n
-            own = lax.dynamic_slice_in_dim(w, me * rows, rows, 1).astype(F32)
-            m_ = 0.9 * m_ + 0.1 * t
-            v_ = 0.95 * v_ + 0.05 * t * t
-            own = (own - 0.02 * (m_ * lax.rsqrt(v_ + 1e-8) + 0.1 * own)).astype(BF16)
-            new[0].append(lax.all_gather(own, "dp", axis=1, tiled=True))
-            new[1].append(m_)
-            new[2].append(v_)
-        return tuple(t for three in new for t in three)
-
+    n = mesh.shape["dp"]
     seq, whole, block = P(("rep", "dp"), None, None), P(None, None, None), P(None, "dp", None)
     return jax.shard_map(
-        step,
+        functools.partial(stepped, n),
         mesh=mesh,
         in_specs=(seq, seq, *[whole] * 3, *[block] * 6),
         out_specs=(*[P("rep", None, None)] * 3, *[P("rep", "dp", None)] * 6),

time: 455 us -> 305 us (0.67)
  waiting for transfers between devices: 239 us -> 0 us
  Pallas kernels: 162 us -> 291 us
  between operations: 16.9 us -> 0.67 us
  blocking collectives: 16.1 us -> 0 us
  other arithmetic: 12.7 us -> 0 us
  local copies, waits for them, and re-layouts: 7.77 us -> 12.8 us
    pallas_call x1, Pallas kernels: 162 us -> 291 us  [stepped(): pl.pallas_call(functools.partial(kernel, n), out_shape=[jax.ShapeDtypeStr...]
    reduce_scatter x3 -> x0, waiting for transfers between devices: 125 us -> none  [step(): lax.psum_scatter(t, 'dp', scatter_dimension=1, tiled=True).astype(F32)]
    all_gather x3 -> x0, waiting for transfers between devices: 113 us -> none  [step(): new[0].append(lax.all_gather(own, 'dp', axis=1, tiled=True))]
    psum x1 -> x0, blocking collectives: 16.1 us -> none  [step(): squares = lax.psum(sum((jnp.sum(t * t) for t in g)), 'dp')]
    convert_element_type x3 -> x0, other arithmetic: 7.36 us -> none  [step(): own = (own - 0.02 * (m_ * lax.rsqrt(v_ + 1e-08) + 0.1 * own)).astype(BF16)]
    reduce_sum x3 -> x0, other arithmetic: 5.31 us -> none  [step(): squares = lax.psum(sum((jnp.sum(t * t) for t in g)), 'dp')]
    unnamed x21 -> x25, local copies, waits for them, and re-layouts: 7.77 us -> 12.8 us
  transfers between devices with their start and end apart: 6 -> 0, of which waited for: 6 -> 0; matrix products, arithmetic and copies ran while one was open for 2% -> 0% of each run, Pallas kernels for 0% -> 0%
where the time goes in v2:
time: 305 us
  Pallas kernels  291 us (95%)
  local copies, waits for them, and re-layouts  12.8 us (4%)
    pallas_call x1, Pallas kernels, stepped(): pl.pallas_call(functools.partial(kernel, n), out_shape=[jax.ShapeDtypeStr...  291 us
    unnamed x25, local copies, waits for them, and re-layouts  12.8 us

profile of v2, /device:TPU:22, one launch (start us, length us, event | category | flops | bytes accessed | tf_op | source)
XLA Modules:
  0.0 304.9 jit_solution(11992616251956556387)
XLA Ops:
  0.6 291.4 %step.1 = (bf16[2,512,1280]{2,1,0:T(8,128)(2,1)}, bf16[2,512,1280]{2,1,0:T(8,128)(2,1)}, bf16[2,1280,512]{2,1,0:T(8,128)(2,1)}, f32[2,64,1280]{2,1,0:T(8,128)}, ...) custom-call(bf16[1,4096,512]{2,1,0:T(8,128)(2,1)} %x_in.1, ...), custom_call_target="tpu_custom_call" | custom-call | tf_op jit(solution)/shard_map/step/pallas_call | solution.py:365
  292.0 0.0 copy-start.1
  292.0 3.6 %copy.29 = bf16[2,512,1280]{2,1,0:T(8,128)(2,1)} copy(bf16[2,512,1280]{2,1,0:T(8,128)(2,1)} %get-tuple-element.18) | data formatting | bytes 5242880
  295.6 0.0 copy-done.1
  295.6 0.0 copy-start
  295.6 1.5 copy.30
  297.1 1.2 copy-done
  298.3 0.0 copy-start.7
  298.3 0.0 copy-start.6
  298.3 1.5 copy.31
  299.8 0.0 copy-done.7
  299.8 0.0 copy-start.5
  299.8 0.0 copy-start.4
  299.8 0.0 copy-start.3
  299.8 0.8 copy.32
  300.7 0.0 copy-done.6
  300.7 0.0 copy-start.2
  300.7 0.8 copy.33
  301.5 0.0 copy-done.5
  301.5 0.8 copy.34
  302.3 0.0 copy-done.4
  302.3 0.8 copy.35
  303.2 0.0 copy-done.3
  303.2 0.8 copy.36
  304.0 0.0 copy-done.2
  304.0 0.8 copy.37
Async XLA Ops:
  292.0 3.6 %copy-start.1 = (bf16[2,512,1280]{2,1,0:T(8,128)(2,1)S(1)}, bf16[2,512,1280]{2,1,0:T(8,128)(2,1)}, u32[]{:S(2)}) copy-start(bf16[2,512,1280]{2,1,0:T(8,128)(2,1)} %get-tuple-element.19) | copy-start | bytes 7864324
  295.6 2.7 copy-start
  298.3 1.5 copy-start.7
  298.3 2.4 copy-start.6
  299.8 1.7 copy-start.5
  299.8 2.5 copy-start.4
  299.8 3.4 %copy-start.3 = (f32[2,64,1280]{2,1,0:T(8,128)S(1)}, f32[2,64,1280]{2,1,0:T(8,128)}, u32[]{:S(2)}) copy-start(f32[2,64,1280]{2,1,0:T(8,128)} %get-tuple-element.25) | copy-start | bytes 1966084
  300.7 3.4 %copy-start.2 = (f32[2,160,512]{2,1,0:T(8,128)S(1)}, f32[2,160,512]{2,1,0:T(8,128)}, u32[]{:S(2)}) copy-start(f32[2,160,512]{2,1,0:T(8,128)} %get-tuple-element.26) | copy-start | bytes 1966084

commit v3 on v2

v3 whole, which is shorter than its diff:
```python
import functools

import jax
import jax.numpy as jnp
from jax import lax
from jax.experimental import pallas as pl
from jax.experimental.pallas import tpu as pltpu
from jax.sharding import PartitionSpec as P

BF16, F32 = jnp.bfloat16, jnp.float32
FB = 256
TF = 512
TB = 1024
SUBS = 4
SETS = 4


def dot(a, b):
    return jnp.dot(a, b, preferred_element_type=F32)


def dot_nt(a, b):
    return lax.dot_general(a, b, (((1,), (1,)), ((), ())), preferred_element_type=F32)


def scale_of(wide):
    return lax.rsqrt(jnp.mean(wide * wide, -1, keepdims=True) + 1e-6)


def sigmoid(g):
    return 0.5 * jnp.tanh(0.5 * g) + 0.5


def forward(ready, x, dy, w, h, a2, a_t, dy_t, hid, da):
    wg, wu, wd = w
    blocks = wg.shape[2] // FB

    def tile(i, _):
        ready(i)
        rows = pl.ds(pl.multiple_of(i * TF, TF), TF)
        wide = x[rows, :].astype(F32)
        a = (wide * scale_of(wide)).astype(BF16)
        for j in range(blocks):
            cols = pl.ds(j * FB, FB)
            gate, up = dot(a, wg[0, :, cols]), dot(a, wu[0, :, cols])
            hid[:, cols] = (gate * sigmoid(gate) * up).astype(BF16)
        out = dot(hid[...], wd[0]).astype(BF16).astype(F32)
        state = (wide + out).astype(BF16)
        h[rows, :] = state
        wide = state.astype(F32)
        n = (wide * scale_of(wide)).astype(BF16)
        a2[rows, :] = n
        a_t[:, rows] = n.T
        dy_t[:, rows] = dy[rows, :].T
        x[rows, :] = a
        da[rows, :] = jnp.zeros((TF, x.shape[1]), F32)
        return 0

    lax.fori_loop(0, x.shape[0] // TF, tile, 0)


def backward_tile(layer, j, i, a_ref, a_t, dy, dy_t, w, acc, da):
    wg, wu, wd = w
    rows = pl.ds(pl.multiple_of(i * TB, TB), TB)
    cols = pl.ds(pl.multiple_of(j * FB, FB), FB)
    hids, dgates, dups = [], [], []
    part = TB // SUBS
    for s in range(SUBS):
        sub = pl.ds(pl.multiple_of(i * TB + s * part, part), part)
        a = a_ref[sub, :]
        gate, up = dot(a, wg[layer, :, cols]), dot(a, wu[layer, :, cols])
        dh = dot_nt(dy[sub, :], wd[layer, cols, :]).astype(BF16).astype(F32)
        sg = sigmoid(gate)
        silu = gate * sg
        hids.append((silu * up).astype(BF16))
        dups.append((dh * silu).astype(BF16))
        dgates.append((dh * up * (sg + silu * (1.0 - sg))).astype(BF16))
    hid, dgate, dup = (jnp.concatenate(t, 0) for t in (hids, dgates, dups))
    acc[0][...] += dot(a_t[:, rows], dgate)
    acc[1][...] += dot(a_t[:, rows], dup)
    acc[2][...] += dot(dy_t[:, rows], hid)
    if da is not None:
        da[rows, :] += dot_nt(dgate, wg[layer, :, cols]) + dot_nt(dup, wu[layer, :, cols])


def between(a1, h, dy, a_t, dy_t, da):
    def tile(i, _):
        rows = pl.ds(pl.multiple_of(i * TF, TF), TF)
        wide = h[rows, :].astype(F32)
        by_a = da[rows, :].astype(BF16).astype(F32)
        scale = scale_of(wide)
        inner = jnp.mean(by_a * wide, -1, keepdims=True)
        by_h = scale * by_a - wide * (scale * scale * scale * inner)
        total = (dy[rows, :].astype(F32) + by_h.astype(BF16).astype(F32)).astype(BF16)
        dy[rows, :] = total
        dy_t[:, rows] = total.T
        a_t[:, rows] = a1[rows, :].T
        return 0

    lax.fori_loop(0, h.shape[0] // TF, tile, 0)


def exchanged(me, n):
    return lax.rem(me + 1, n), lax.rem(me + n - 1, n)


def remote(src, dst, send, recv, to):
    return pltpu.make_async_remote_copy(
        src_ref=src, dst_ref=dst, send_sem=send, recv_sem=recv, device_id={"dp": to}, device_id_type=pl.DeviceIdType.MESH
    )


class Chain:
    def __init__(self, terms, slots, send, recv, long, rows, me, n):
        self.terms, self.slots, self.send, self.recv, self.long = terms, slots, send, recv, long
        self.rows, self.me, self.n = rows, me, n

    def hops(self, way):
        return self.n // 2 - (way != self.long)

    def chunk(self, far):
        stride, first, size = self.rows
        at = lax.rem(self.me + self.n + far, self.n)
        return pl.ds(pl.multiple_of(at * stride, size) + first, size)

    def going(self, way, hop):
        left = self.hops(way) - hop
        return self.chunk(left if way == 0 else -left)

    def slot(self, way, hop):
        return hop + (way != self.long) * (self.n // 2)

    def copy(self, way, hop):
        k = self.slot(way, hop)
        return remote(
            self.terms.at[self.going(way, hop), :], self.slots.at[k], self.send.at[k], self.recv.at[k], exchanged(self.me, self.n)[way]
        )

    def step(self, s):
        for way in range(2):
            if 0 < s <= self.hops(way):
                self.copy(way, s - 1).wait()
            if s < self.hops(way):
                if s:
                    self.add(self.going(way, s), self.slot(way, s - 1))
                self.copy(way, s).start()
        if s == self.n // 2:
            self.add(self.chunk(0), *(self.slot(way, self.hops(way) - 1) for way in range(2)))

    def add(self, at, *slots):
        total = self.terms[at, :].astype(F32)
        for k in slots:
            total += self.slots[k].astype(F32)
        self.terms[at, :] = total.astype(BF16)


def kernel(n, x_in, dy_in, wg_in, wu_in, wd_in, mg_in, mu_in, md_in, vg_in, vu_in, vd_in,
           og, ou, od, mg_out, mu_out, md_out, vg_out, vu_out, vd_out,
           x, dy, wg, wu, wd, h, a2, a_t, dy_t, hid, da, ag, au, ad,
           tg, tu, td, slot_gu, slot_d, mg, mu, md, vg, vu, vd, ng, nu, nd, mine, others,
           sems, xsems, msems, rs_send, rs_recv, rd_send, rd_recv, sq_send, sq_recv, ag_send, ag_recv, osems):
    me = lax.axis_index("dp")
    layers, d, ff = wg.shape
    blocks = ff // FB
    ticks = n // 2
    pieces = layers * blocks
    first = [
        pltpu.make_async_copy(src.at[layer], dst.at[layer], sems.at[k, layer])
        for layer in range(layers)
        for k, (src, dst) in enumerate(((wg_in, wg), (wu_in, wu), (wd_in, wd)))
    ]

    def tokens(i):
        rows = pl.ds(pl.multiple_of(i * TF, TF), TF)
        return [pltpu.make_async_copy(src.at[0, rows, :], dst.at[rows, :], xsems.at[k, i]) for k, (src, dst) in enumerate(((x_in, x), (dy_in, dy)))]

    tiles = x.shape[0] // TF
    for c in first[:3] + [c for i in range(tiles) for c in tokens(i)] + first[3:]:
        c.start()
    moments = (mg, mu, md, vg, vu, vd)
    later = [
        pltpu.make_async_copy(src, dst, msems.at[k])
        for k, (src, dst) in enumerate(zip((mg_in, mu_in, md_in, vg_in, vu_in, vd_in), moments, strict=True))
    ]
    for c in later:
        c.start()
    barrier = pltpu.get_barrier_semaphore()
    for off in range(1, n):
        pl.semaphore_signal(barrier, 1, device_id={"dp": lax.rem(me + off, n)}, device_id_type=pl.DeviceIdType.MESH)
    for c in first[:3]:
        c.wait()
    w, acc = (wg, wu, wd), (ag, au, ad)

    def ready(i):
        for c in tokens(i):
            c.wait()

    forward(ready, x, dy, w, h, a2, a_t, dy_t, hid, da)
    for c in first[3:]:
        c.wait()
    pl.semaphore_wait(barrier, n - 1)

    per, per_d = d // n, ff // n
    half = per_d // 2

    def piece(p, s):
        k = lax.rem(p, SETS)
        for which, terms in enumerate((tg, tu)):
            Chain(terms.at[p], slot_gu.at[k, which], rs_send.at[k, which], rs_recv.at[k, which], which, (per, 0, per), me, n).step(s)

    def piece_d(layer, part, s):
        k = layer * 2 + part
        for which in range(2):
            rows = (per_d, part * half, half)
            Chain(td.at[layer, which], slot_d.at[k, which], rd_send.at[k, which], rd_recv.at[k, which], which, rows, me, n).step(s)

    def at_tick(i, tick, p, back, s):
        @pl.when(jnp.logical_and(i == tick, jnp.logical_and(p >= back, p < pieces + back)))
        def _():
            piece(p - back, s)

    def tick(p, i):
        at_tick(i, 0, p, 1, 0)
        at_tick(i, 1, p, 2, 2)
        at_tick(i, 1, p, 3, 4)
        at_tick(i, 2, p, 1, 1)
        at_tick(i, 3, p, 2, 3)

    def tick_d(k):
        for s in range(n // 2 + 1):
            for part in range(2):

                @pl.when(k == 4 * s + 2 * part)
                def _(s=s, part=part):
                    piece_d(1, part, s)

    def backward(layer, first, a_ref, da):
        def block(j, _):
            p = first + j
            for to in acc:
                to[...] = jnp.zeros_like(to)

            def tile(i, _):
                tick(p, i)
                if first:
                    tick_d(j * ticks + i)
                backward_tile(layer, j, i, a_ref, a_t, dy, dy_t, w, acc, da)
                return 0

            lax.fori_loop(0, ticks, tile, 0)
            tg[p] = ag[...].astype(BF16)
            tu[p] = au[...].astype(BF16)
            rows = pl.ds(pl.multiple_of(j * FB, FB), FB)
            by_down = ad[...].astype(BF16).T
            td[layer, 0, rows, :] = by_down[:, : d // 2]
            td[layer, 1, rows, :] = by_down[:, d // 2 :]
            return 0

        lax.fori_loop(0, blocks, block, 0)

    backward(1, 0, a2, da)
    between(x, h, dy, a_t, dy_t, da)
    backward(0, blocks, x, None)

    end = pieces - 1
    for s in range(n // 2 + 1):
        piece(end, s)
        for part in range(2):
            piece_d(0, part, s)
        if s == 0:
            piece(end - 1, 2)
            piece(end - 2, 4)
        elif s < 3:
            piece(end - 1, s + 2)

    own, own_d = pl.ds(pl.multiple_of(me * per, per), per), pl.ds(pl.multiple_of(me * per_d, per_d), per_d)
    total = jnp.zeros((8, 128), F32)

    def squares(t):
        t = t.astype(F32)
        return jnp.sum(t * t)

    local = jnp.float32(0)
    for p in range(pieces):
        local += squares(tg[p, own, :]) + squares(tu[p, own, :])
    for layer in range(layers):
        for way in range(2):
            local += squares(td[layer, way, own_d, :])
    mine[...] = total + local
    sent = [remote(mine, others.at[k - 1], sq_send.at[k - 1], sq_recv.at[k - 1], lax.rem(me + k, n)) for k in range(1, n)]
    for c in sent:
        c.start()
    for c in later:
        c.wait()
    for c in sent:
        c.wait()
    summed = mine[...]
    for k in range(n - 1):
        summed = summed + others[k]
    count = layers * d * ff * 3
    factor = jnp.minimum(1.0, 0.5 * lax.rsqrt(summed[0:1, 0:1] / count + 1e-30))

    def adamw(w_own, m_at, v_at, g, new):
        g = g.astype(F32) * factor
        m_ = 0.9 * m_at[...] + 0.1 * g
        v_ = 0.95 * v_at[...] + 0.05 * g * g
        m_at[...] = m_
        v_at[...] = v_
        w_own = w_own.astype(F32)
        new[...] = (w_own - 0.02 * (m_ * lax.rsqrt(v_ + 1e-8) + 0.1 * w_own)).astype(BF16)

    outs, news, owns = (og, ou, od), (ng, nu, nd), (own, own, own_d)

    def gather(kind, layer, way, hop):
        far = lax.rem(me + n - hop, n) if way == 0 else lax.rem(me + hop, n)
        size = per_d if kind == 2 else per
        rows = outs[kind].at[layer, pl.ds(pl.multiple_of(far * size, size), size), :]
        k = hop + (way != layer % 2) * (n // 2)
        src = rows if hop else news[kind].at[layer]
        return remote(src, rows, ag_send.at[layer, kind, k], ag_recv.at[layer, kind, k], exchanged(me, n)[way])

    def hops(layer, way):
        return n // 2 - (way != layer % 2)

    finals = []
    for kind in range(3):
        for layer in range(layers):
            if kind < 2:
                for j in range(blocks):
                    cols = pl.ds(j * FB, FB)
                    adamw(
                        w[kind][layer, own, cols],
                        (mg, mu)[kind].at[layer, :, cols],
                        (vg, vu)[kind].at[layer, :, cols],
                        (tg, tu)[kind][(layers - 1 - layer) * blocks + j, own, :],
                        news[kind].at[layer, :, cols],
                    )
            else:
                for way in range(2):
                    cols = pl.ds(way * (d // 2), d // 2)
                    adamw(wd[layer, own_d, cols], md.at[layer, :, cols], vd.at[layer, :, cols], td[layer, way, own_d, :], nd.at[layer, :, cols])
            for way in range(2):
                gather(kind, layer, way, 0).start()
        finals.append(pltpu.make_async_copy(news[kind], outs[kind].at[:, owns[kind], :], osems.at[kind]))
        finals.append(pltpu.make_async_copy(moments[kind], (mg_out, mu_out, md_out)[kind], osems.at[3 + kind]))
        finals.append(pltpu.make_async_copy(moments[3 + kind], (vg_out, vu_out, vd_out)[kind], osems.at[6 + kind]))
        for c in finals[-3:]:
            c.start()
    for hop in range(1, n // 2 + 1):
        for kind in range(3):
            for layer in range(layers):
                for way in range(2):
                    if hop <= hops(layer, way):
                        gather(kind, layer, way, hop - 1).wait()
                    if hop < hops(layer, way):
                        gather(kind, layer, way, hop).start()
    for c in finals:
        c.wait()


def stepped(n, x, dy, *arrays):
    _, t, d = x.shape
    wg, _, wd = arrays[:3]
    layers, _, ff = wg.shape
    per, per_d = d // n, ff // n
    pieces = layers * (ff // FB)
    any_ = pl.BlockSpec(memory_space=pl.ANY)
    dma = pltpu.SemaphoreType.DMA
    return pl.pallas_call(
        functools.partial(kernel, n),
        out_shape=[jax.ShapeDtypeStruct(a.shape, a.dtype) for a in arrays],
        in_specs=[any_] * 11,
        out_specs=[any_] * 9,
        scratch_shapes=[
            pltpu.VMEM((t, d), BF16),
            pltpu.VMEM((t, d), BF16),
            *[pltpu.VMEM(w.shape, BF16) for w in arrays[:3]],
            pltpu.VMEM((t, d), BF16),
            pltpu.VMEM((t, d), BF16),
            pltpu.VMEM((d, t), BF16),
            pltpu.VMEM((d, t), BF16),
            pltpu.VMEM((TF, ff), BF16),
            pltpu.VMEM((t, d), F32),
            *[pltpu.VMEM((d, FB), F32)] * 3,
            *[pltpu.VMEM((pieces, d, FB), BF16)] * 2,
            pltpu.VMEM((layers, 2, ff, d // 2), BF16),
            pltpu.VMEM((SETS, 2, n - 1, per, FB), BF16),
            pltpu.VMEM((layers * 2, 2, n - 1, per_d // 2, d // 2), BF16),
            *[pltpu.VMEM(a.shape, F32) for a in arrays[3:]],
            *[pltpu.VMEM(a.shape, BF16) for a in arrays[3:6]],
            pltpu.VMEM((8, 128), F32),
            pltpu.VMEM((n - 1, 8, 128), F32),
            dma((3, layers)),
            dma((2, t // TF)),
            dma((6,)),
            dma((SETS, 2, n - 1)),
            dma((SETS, 2, n - 1)),
            dma((layers * 2, 2, n - 1)),
            dma((layers * 2, 2, n - 1)),
            dma((n - 1,)),
            dma((n - 1,)),
            dma((layers, 3, n - 1)),
            dma((layers, 3, n - 1)),
            dma((9,)),
        ],
        compiler_params=pltpu.CompilerParams(vmem_limit_bytes=67_043_328, collective_id=0, has_side_effects=True),
        name="step",
    )(x, dy, *arrays)


def handed_over(*refs):
    count = len(refs) // 2
    writes = [pltpu.make_async_copy(refs[k], refs[count + k], refs[-1].at[k]) for k in range(count)]
    for c in writes:
        c.start()
    for c in writes:
        c.wait()


def both(n, *arrays):
    results = stepped(n, *arrays)
    parts = len(results)
    return pl.pallas_call(
        handed_over,
        out_shape=[jax.ShapeDtypeStruct(r.shape, r.dtype) for r in results],
        in_specs=[pl.BlockSpec(memory_space=pltpu.VMEM)] * parts,
        out_specs=[pl.BlockSpec(memory_space=pl.ANY)] * parts,
        scratch_shapes=[pltpu.SemaphoreType.DMA((parts,))],
        compiler_params=pltpu.CompilerParams(vmem_limit_bytes=32_000_000),
        name="hand_over",
    )(*results)


def solution(mesh):
    n = mesh.shape["dp"]
    seq, whole, block = P(("rep", "dp"), None, None), P(None, None, None), P(None, "dp", None)
    return jax.shard_map(
        functools.partial(both, n),
        mesh=mesh,
        in_specs=(seq, seq, *[whole] * 3, *[block] * 6),
        out_specs=(*[P("rep", None, None)] * 3, *[P("rep", "dp", None)] * 6),
        check_vma=False,
    )
```

time: 305 us -> 256 us (0.84)
  Pallas kernels: 291 us -> 243 us
    pallas_call x1, Pallas kernels: 291 us -> 238 us  [stepped(): pl.pallas_call(functools.partial(kernel, n), out_shape=[jax.ShapeDtypeStr...]
    pallas_call x0 -> x1, Pallas kernels: none -> 4.41 us  [both(): pl.pallas_call(handed_over, out_shape=[jax.ShapeDtypeStruct(r.shape, r.dt...]
    unnamed x25 -> x18, local copies, waits for them, and re-layouts: 12.8 us -> 11.7 us
where the time goes in v3:
time: 256 us; the launch traced here: 255 us
  Pallas kernels  243 us (95%)
  local copies, waits for them, and re-layouts  11.7 us (5%)
    pallas_call x1, Pallas kernels, stepped(): pl.pallas_call(functools.partial(kernel, n), out_shape=[jax.ShapeDtypeStr...  238 us
    unnamed x18, local copies, waits for them, and re-layouts  11.7 us

profile of v3, /device:TPU:22, one launch (start us, length us, event | category | flops | bytes accessed | tf_op | source)
XLA Modules:
  0.0 255.2 jit_solution(16375243395530397237)
XLA Ops:
  0.6 238.2 %step.1 = (bf16[2,512,1280]{2,1,0:T(8,128)(2,1)}, bf16[2,512,1280]{2,1,0:T(8,128)(2,1)}, bf16[2,1280,512]{2,1,0:T(8,128)(2,1)}, f32[2,64,1280]{2,1,0:T(8,128)}, ...) custom-call(bf16[1,4096,512]{2,1,0:T(8,128)(2,1)} %x_in.1, ...), custom_call_target="tpu_custom_call" | custom-call | tf_op jit(solution)/shard_map/step/pallas_call | solution.py:369
  238.9 0.0 copy-start
  238.9 1.7 copy-done
  240.6 0.0 copy-start.1
  240.6 1.7 copy-done.1
  242.3 0.0 copy-start.2
  242.4 1.7 copy-done.2
  244.1 0.0 copy-start.3
  244.1 1.1 copy-done.3
  245.2 0.0 copy-start.4
  245.2 1.1 copy-done.4
  246.3 0.0 copy-start.5
  246.3 1.1 copy-done.5
  247.4 0.0 copy-start.6
  247.4 1.1 copy-done.6
  248.4 0.0 copy-start.7
  248.4 1.1 copy-done.7
  249.5 0.0 copy-start.8
  249.5 1.1 copy-done.8
  250.6 4.4 %hand_over.1 = (bf16[2,512,1280]{2,1,0:T(8,128)(2,1)}, bf16[2,512,1280]{2,1,0:T(8,128)(2,1)}, bf16[2,1280,512]{2,1,0:T(8,128)(2,1)}, f32[2,64,1280]{2,1,0:T(8,12...) custom-call(bf16[2,512,1280]{2,1,0:T(8,128)(2,1)S(1)} %copy-done, ...), custom_call_target="tpu_custom_call" | custom-call | tf_op jit(solution)/shard_map/hand_over/pallas_call | solution.py:423
Async XLA Ops:
  238.9 1.7 copy-start
  240.6 1.7 copy-start.1
  242.3 1.7 copy-start.2
  244.1 1.1 copy-start.3
  245.2 1.1 copy-start.4
  246.3 1.1 copy-start.5
  247.4 1.1 copy-start.6
  248.4 1.1 copy-start.7
  249.5 1.1 copy-start.8

commit v4 on v3

v4 whole, which is shorter than its diff:
```python
import functools

import jax
import jax.numpy as jnp
from jax import lax
from jax.experimental import pallas as pl
from jax.experimental.pallas import tpu as pltpu
from jax.sharding import PartitionSpec as P

BF16, F32 = jnp.bfloat16, jnp.float32
FB = 256
TF = 512
TB = 1024
SUBS = 4
SETS = 4


def dot(a, b):
    return jnp.dot(a, b, preferred_element_type=F32)


def dot_nt(a, b):
    return lax.dot_general(a, b, (((1,), (1,)), ((), ())), preferred_element_type=F32)


def scale_of(wide):
    return lax.rsqrt(jnp.mean(wide * wide, -1, keepdims=True) + 1e-6)


def sigmoid(g):
    return 0.5 * jnp.tanh(0.5 * g) + 0.5


def grouped(t, n):
    own = t.shape[1] // n
    size = FB // n
    return jnp.concatenate([t[:, own * k + size * j : own * k + size * (j + 1)] for j in range(own // size) for k in range(n)], 1)


def ungrouped(blocks, n):
    size = FB // n
    return jnp.concatenate([t[:, size * k : size * (k + 1)] for k in range(n) for t in blocks], 1)


def forward(n, wg0, wu0, ready, x, dy, w, h, a2, a_t, dy_t, hid, da):
    wg, wu, wd = w
    blocks = wg.shape[2] // FB
    share = wg.shape[1] // (x.shape[0] // TF)

    def tile(i, _):
        ready(i)
        rows = pl.ds(pl.multiple_of(i * TF, TF), TF)
        wide = x[rows, :].astype(F32)
        a = (wide * scale_of(wide)).astype(BF16)
        for j in range(blocks):
            cols = pl.ds(j * FB, FB)
            gate, up = dot(a, wg[0, :, cols]), dot(a, wu[0, :, cols])
            hid[:, cols] = (gate * sigmoid(gate) * up).astype(BF16)
        out = dot(hid[...], wd[0]).astype(BF16).astype(F32)
        state = (wide + out).astype(BF16)
        h[rows, :] = state
        wide = state.astype(F32)
        normed = (wide * scale_of(wide)).astype(BF16)
        a2[rows, :] = normed
        a_t[:, rows] = normed.T
        dy_t[:, rows] = dy[rows, :].T
        x[rows, :] = a
        da[rows, :] = jnp.zeros((TF, x.shape[1]), F32)
        some = pl.ds(pl.multiple_of(i * share, share), share)
        for natural, new in zip((wg, wu), (wg0, wu0), strict=True):
            new[some, :] = grouped(natural[0, some, :], n)
            natural[1, some, :] = grouped(natural[1, some, :], n)
        return 0

    lax.fori_loop(0, x.shape[0] // TF, tile, 0)


def backward_tile(j, i, a_ref, a_t, dy, dy_t, w, acc, da):
    wg, wu, wd = w
    rows = pl.ds(pl.multiple_of(i * TB, TB), TB)
    cols = pl.ds(pl.multiple_of(j * FB, FB), FB)
    hids, dgates, dups = [], [], []
    part = TB // SUBS
    for s in range(SUBS):
        sub = pl.ds(pl.multiple_of(i * TB + s * part, part), part)
        a = a_ref[sub, :]
        gate, up = dot(a, wg[:, cols]), dot(a, wu[:, cols])
        dh = dot_nt(dy[sub, :], wd[cols, :]).astype(BF16).astype(F32)
        sg = sigmoid(gate)
        silu = gate * sg
        hids.append((silu * up).astype(BF16))
        dups.append((dh * silu).astype(BF16))
        dgates.append((dh * up * (sg + silu * (1.0 - sg))).astype(BF16))
    hid, dgate, dup = (jnp.concatenate(t, 0) for t in (hids, dgates, dups))
    acc[0][...] += dot(a_t[:, rows], dgate)
    acc[1][...] += dot(a_t[:, rows], dup)
    acc[2][...] += dot(dy_t[:, rows], hid)
    if da is not None:
        da[rows, :] += dot_nt(dgate, wg[:, cols]) + dot_nt(dup, wu[:, cols])


def between(i, a1, h, dy, a_t, dy_t, da):
    for part in range(TB // TF):
        rows = pl.ds(pl.multiple_of(i * TB + part * TF, TF), TF)
        wide = h[rows, :].astype(F32)
        by_a = da[rows, :].astype(BF16).astype(F32)
        scale = scale_of(wide)
        inner = jnp.mean(by_a * wide, -1, keepdims=True)
        by_h = scale * by_a - wide * (scale * scale * scale * inner)
        total = (dy[rows, :].astype(F32) + by_h.astype(BF16).astype(F32)).astype(BF16)
        dy[rows, :] = total
        dy_t[:, rows] = total.T
        a_t[:, rows] = a1[rows, :].T


def exchanged(me, n):
    return lax.rem(me + 1, n), lax.rem(me + n - 1, n)


def remote(src, dst, send, recv, to):
    return pltpu.make_async_remote_copy(
        src_ref=src, dst_ref=dst, send_sem=send, recv_sem=recv, device_id={"dp": to}, device_id_type=pl.DeviceIdType.MESH
    )


class Chain:
    def __init__(self, terms, slots, send, recv, long, me, n):
        self.terms, self.slots, self.send, self.recv, self.long, self.me, self.n = terms, slots, send, recv, long, me, n

    def hops(self, way):
        return self.n // 2 - (way != self.long)

    def chunk(self, far):
        return lax.rem(self.me + self.n + far, self.n)

    def going(self, way, hop):
        left = self.hops(way) - hop
        return self.chunk(left if way == 0 else -left)

    def slot(self, way, hop):
        return hop + (way != self.long) * (self.n // 2)

    def copy(self, way, hop):
        k = self.slot(way, hop)
        return remote(
            self.terms.at[self.going(way, hop)], self.slots.at[k], self.send.at[k], self.recv.at[k], exchanged(self.me, self.n)[way]
        )

    def step(self, s):
        for way in range(2):
            if 0 < s <= self.hops(way):
                self.copy(way, s - 1).wait()
            if s < self.hops(way):
                if s:
                    self.add(self.going(way, s), self.slot(way, s - 1))
                self.copy(way, s).start()
        if s == self.n // 2:
            self.add(self.chunk(0), *(self.slot(way, self.hops(way) - 1) for way in range(2)))

    def add(self, at, *slots):
        total = self.terms[at].astype(F32)
        for k in slots:
            total += self.slots[k].astype(F32)
        self.terms[at] = total.astype(BF16)


def kernel(n, x_in, dy_in, wg_in, wu_in, wd_in, mg_in, mu_in, md_in, vg_in, vu_in, vd_in,
           og, ou, od, mg_out, mu_out, md_out, vg_out, vu_out, vd_out,
           x, dy, wg, wu, wd, h, a2, a_t, dy_t, hid, da, ag, au, ad,
           wg0, wu0, t0, t1, slots, mg, mu, md, vg, vu, vd, ng, nu, nd, mine, others,
           sems, xsems, gsems, msems, rs_send, rs_recv, sq_send, sq_recv, ag_send, ag_recv, osems):
    me = lax.axis_index("dp")
    layers, d, ff = wg.shape
    blocks = ff // FB
    ticks = n // 2
    per, per_d, part_d = d // n, ff // n, FB // n
    pieces = layers * blocks
    def load(which, layer):
        src, dst = ((wg_in, wg), (wu_in, wu), (wd_in, wd))[which]
        return pltpu.make_async_copy(src.at[layer], dst.at[layer], sems.at[which, layer])

    def load_grouped(layer):
        def one(k, _):
            to, j = k // blocks, lax.rem(k, blocks)
            src = pl.ds(pl.multiple_of(to * per_d + j * part_d, part_d), part_d)
            dst = pl.ds(pl.multiple_of(j * FB + to * part_d, part_d), part_d)
            pltpu.make_async_copy(wd_in.at[layer, src, :], wd.at[layer, dst, :], gsems.at[layer]).start()
            return 0

        lax.fori_loop(0, n * blocks, one, 0)

    def grouped_loaded(layer):
        pltpu.make_async_copy(wd_in.at[layer], wd.at[layer], gsems.at[layer]).wait()

    def tokens(i):
        rows = pl.ds(pl.multiple_of(i * TF, TF), TF)
        return [pltpu.make_async_copy(src.at[0, rows, :], dst.at[rows, :], xsems.at[k, i]) for k, (src, dst) in enumerate(((x_in, x), (dy_in, dy)))]

    tiles = x.shape[0] // TF
    before = [load(0, 0), load(1, 0), load(2, 0), load(0, 1), load(1, 1)]
    for c in before[:3] + tokens(0) + before[3:] + [c for i in range(1, tiles) for c in tokens(i)]:
        c.start()
    load_grouped(1)
    moments = (mg, mu, md, vg, vu, vd)
    later = [
        pltpu.make_async_copy(src, dst, msems.at[k])
        for k, (src, dst) in enumerate(zip((mg_in, mu_in, md_in, vg_in, vu_in, vd_in), moments, strict=True))
    ]
    own, own_d = pl.ds(pl.multiple_of(me * per, per), per), pl.ds(pl.multiple_of(me * per_d, per_d), per_d)
    owned = ((wg_in, own, ng), (wu_in, own, nu), (wd_in, own_d, nd))
    later += [pltpu.make_async_copy(src.at[:, at, :], dst, msems.at[6 + k]) for k, (src, at, dst) in enumerate(owned)]
    for c in later:
        c.start()
    barrier = pltpu.get_barrier_semaphore()
    for off in range(1, n):
        pl.semaphore_signal(barrier, 1, device_id={"dp": lax.rem(me + off, n)}, device_id_type=pl.DeviceIdType.MESH)
    for c in before:
        c.wait()
    w, acc = (wg, wu, wd), (ag, au, ad)

    def ready(i):
        for c in tokens(i):
            c.wait()

    forward(n, wg0, wu0, ready, x, dy, w, h, a2, a_t, dy_t, hid, da)
    load_grouped(0)
    grouped_loaded(1)
    pl.semaphore_wait(barrier, n - 1)


    def piece(p, s):
        k = lax.rem(p, SETS)
        for which, terms in enumerate((t0, t1)):
            Chain(terms.at[p], slots.at[k, which], rs_send.at[k, which], rs_recv.at[k, which], which, me, n).step(s)

    def at_tick(i, tick, p, back, s):
        @pl.when(jnp.logical_and(i == tick, jnp.logical_and(p >= back, p < pieces + back)))
        def _():
            piece(p - back, s)

    def tick(p, i):
        at_tick(i, 0, p, 1, 0)
        at_tick(i, 1, p, 2, 2)
        at_tick(i, 1, p, 3, 4)
        at_tick(i, 2, p, 1, 1)
        at_tick(i, 3, p, 2, 3)

    da_all = da

    def backward(layer, first, a_ref, da):
        of_layer = (wg0, wu0, wd.at[0]) if layer == 0 else (wg.at[1], wu.at[1], wd.at[1])

        def block(j, _, fresh=False):
            p = first + j
            for to in acc:
                to[...] = jnp.zeros_like(to)

            def tile(i, _):
                tick(p, i)
                if fresh:
                    between(i, x, h, dy, a_t, dy_t, da_all)
                backward_tile(j, i, a_ref, a_t, dy, dy_t, of_layer, acc, da)
                return 0

            lax.fori_loop(0, ticks, tile, 0)
            by_down = ad[...].astype(BF16).T
            for terms, of_in, of_down in ((t0, ag, by_down[:, : d // 2]), (t1, au, by_down[:, d // 2 :])):
                terms[p, :, :per, :] = of_in[...].astype(BF16).reshape(n, per, FB)
                terms[p, :, per:, :] = of_down.reshape(n, part_d, FB)
            return 0

        if layer == 0:
            block(0, 0, True)
        lax.fori_loop(1 if layer == 0 else 0, blocks, block, 0)

    backward(1, 0, a2, da)
    grouped_loaded(0)
    backward(0, blocks, x, None)

    def squares(p):
        return sum(jnp.sum(t * t) for t in (terms[p, me].astype(F32) for terms in (t0, t1)))

    end = pieces - 1
    local = jnp.float32(0)
    for s in range(n // 2 + 1):
        piece(end, s)
        if s == 0:
            piece(end - 1, 2)
            piece(end - 2, 4)
        elif s < 3:
            piece(end - 1, s + 2)
        elif s == 3:
            local += sum(squares(p) for p in range(end))

    local += squares(end)
    total = jnp.zeros((8, 128), F32)
    mine[...] = total + local
    sent = [remote(mine, others.at[k - 1], sq_send.at[k - 1], sq_recv.at[k - 1], lax.rem(me + k, n)) for k in range(1, n)]
    for c in sent:
        c.start()
    for c in later:
        c.wait()
    for c in sent:
        c.wait()
    summed = mine[...]
    for k in range(n - 1):
        summed = summed + others[k]
    count = layers * d * ff * 3
    factor = jnp.minimum(1.0, 0.5 * lax.rsqrt(summed[0:1, 0:1] / count + 1e-30))

    def adamw(m_at, v_at, g, new):
        g = g.astype(F32) * factor
        m_ = 0.9 * m_at[...] + 0.1 * g
        v_ = 0.95 * v_at[...] + 0.05 * g * g
        m_at[...] = m_
        v_at[...] = v_
        old = new[...].astype(F32)
        new[...] = (old - 0.02 * (m_ * lax.rsqrt(v_ + 1e-8) + 0.1 * old)).astype(BF16)

    outs, news, owns = (og, ou, od), (ng, nu, nd), (own, own, own_d)

    def gather(kind, layer, way, hop):
        far = lax.rem(me + n - hop, n) if way == 0 else lax.rem(me + hop, n)
        size = per_d if kind == 2 else per
        rows = outs[kind].at[layer, pl.ds(pl.multiple_of(far * size, size), size), :]
        k = hop + (way != layer % 2) * (n // 2)
        src = rows if hop else news[kind].at[layer]
        return remote(src, rows, ag_send.at[layer, kind, k], ag_recv.at[layer, kind, k], exchanged(me, n)[way])

    def hops(layer, way):
        return n // 2 - (way != layer % 2)

    finals = []
    for kind in range(3):
        for layer in range(layers):
            of = range((layers - 1 - layer) * blocks, (layers - layer) * blocks)
            m_at, v_at, new = (t.at[layer] for t in (moments[kind], moments[3 + kind], news[kind]))
            if kind < 2:
                adamw(m_at, v_at, ungrouped([(t0, t1)[kind][p, me, :per, :] for p in of], n), new)
            else:
                for j, p in enumerate(of):
                    for way in range(2):
                        at = pl.ds(j * part_d, part_d), pl.ds(way * (d // 2), d // 2)
                        adamw(m_at.at[at], v_at.at[at], (t0, t1)[way][p, me, per:, :], new.at[at])
            for way in range(2):
                gather(kind, layer, way, 0).start()
        finals.append(pltpu.make_async_copy(news[kind], outs[kind].at[:, owns[kind], :], osems.at[kind]))
        finals.append(pltpu.make_async_copy(moments[kind], (mg_out, mu_out, md_out)[kind], osems.at[3 + kind]))
        finals.append(pltpu.make_async_copy(moments[3 + kind], (vg_out, vu_out, vd_out)[kind], osems.at[6 + kind]))
        for c in finals[-3:]:
            c.start()
    for hop in range(1, n // 2 + 1):
        for kind in range(3):
            for layer in range(layers):
                for way in range(2):
                    if hop <= hops(layer, way):
                        gather(kind, layer, way, hop - 1).wait()
                    if hop < hops(layer, way):
                        gather(kind, layer, way, hop).start()
    for c in finals:
        c.wait()


def stepped(n, x, dy, *arrays):
    _, t, d = x.shape
    wg, _, wd = arrays[:3]
    layers, _, ff = wg.shape
    per = d // n
    pieces = layers * (ff // FB)
    any_ = pl.BlockSpec(memory_space=pl.ANY)
    dma = pltpu.SemaphoreType.DMA
    return pl.pallas_call(
        functools.partial(kernel, n),
        out_shape=[jax.ShapeDtypeStruct(a.shape, a.dtype) for a in arrays],
        in_specs=[any_] * 11,
        out_specs=[any_] * 9,
        scratch_shapes=[
            pltpu.VMEM((t, d), BF16),
            pltpu.VMEM((t, d), BF16),
            *[pltpu.VMEM(w.shape, BF16) for w in arrays[:3]],
            pltpu.VMEM((t, d), BF16),
            pltpu.VMEM((t, d), BF16),
            pltpu.VMEM((d, t), BF16),
            pltpu.VMEM((d, t), BF16),
            pltpu.VMEM((TF, ff), BF16),
            pltpu.VMEM((t, d), F32),
            *[pltpu.VMEM((d, FB), F32)] * 3,
            *[pltpu.VMEM((d, ff), BF16)] * 2,
            *[pltpu.VMEM((pieces, n, per + FB // n, FB), BF16)] * 2,
            pltpu.VMEM((SETS, 2, n - 1, per + FB // n, FB), BF16),
            *[pltpu.VMEM(a.shape, F32) for a in arrays[3:]],
            *[pltpu.VMEM(a.shape, BF16) for a in arrays[3:6]],
            pltpu.VMEM((8, 128), F32),
            pltpu.VMEM((n - 1, 8, 128), F32),
            dma((3, layers)),
            dma((2, t // TF)),
            dma((layers,)),
            dma((9,)),
            dma((SETS, 2, n - 1)),
            dma((SETS, 2, n - 1)),
            dma((n - 1,)),
            dma((n - 1,)),
            dma((layers, 3, n - 1)),
            dma((layers, 3, n - 1)),
            dma((9,)),
        ],
        compiler_params=pltpu.CompilerParams(vmem_limit_bytes=67_043_328, collective_id=0, has_side_effects=True),
        name="step",
    )(x, dy, *arrays)


def handed_over(*refs):
    count = (len(refs) - 1) // 3
    steps = [(layer, k) for k in range(count) for layer in range(refs[k].shape[0])]
    sems = refs[-1]

    def copy(which, layer, k):
        return pltpu.make_async_copy(
            refs[k + (0, 2)[which] * count].at[layer], refs[k + (2, 1)[which] * count].at[layer], sems.at[which, k, layer]
        )

    for at in steps:
        copy(0, *at).start()
    for at in steps:
        copy(0, *at).wait()
        copy(1, *at).start()
    for at in steps:
        copy(1, *at).wait()


def both(n, *arrays):
    results = stepped(n, *arrays)
    parts = len(results)
    any_ = pl.BlockSpec(memory_space=pl.ANY)
    return pl.pallas_call(
        handed_over,
        out_shape=[jax.ShapeDtypeStruct(r.shape, r.dtype) for r in results],
        in_specs=[any_] * parts,
        out_specs=[any_] * parts,
        scratch_shapes=[*[pltpu.VMEM(r.shape, r.dtype) for r in results], pltpu.SemaphoreType.DMA((2, parts, results[0].shape[0]))],
        compiler_params=pltpu.CompilerParams(vmem_limit_bytes=67_043_328),
        name="hand_over",
    )(*results)


def solution(mesh):
    n = mesh.shape["dp"]
    seq, whole, block = P(("rep", "dp"), None, None), P(None, None, None), P(None, "dp", None)
    return jax.shard_map(
        functools.partial(both, n),
        mesh=mesh,
        in_specs=(seq, seq, *[whole] * 3, *[block] * 6),
        out_specs=(*[P("rep", None, None)] * 3, *[P("rep", "dp", None)] * 6),
        check_vma=False,
    )
```

time: 256 us -> 239 us (0.934)
  local copies, waits for them, and re-layouts: 11.7 us -> 0 us
  Pallas kernels: 243 us -> 238 us
    unnamed x18 -> x0, local copies, waits for them, and re-layouts: 11.7 us -> none
    pallas_call x1, Pallas kernels: 238 us -> 229 us  [stepped(): pl.pallas_call(functools.partial(kernel, n), out_shape=[jax.ShapeDtypeStr...]
    pallas_call x1, Pallas kernels: 4.41 us -> 9.12 us  [both(): pl.pallas_call(handed_over, out_shape=[jax.ShapeDtypeStruct(r.shape, r.dt...]
where the time goes in v4:
time: 239 us
  Pallas kernels  238 us (100%)
    pallas_call x1, Pallas kernels, stepped(): pl.pallas_call(functools.partial(kernel, n), out_shape=[jax.ShapeDtypeStr...  229 us
    pallas_call x1, Pallas kernels, both(): pl.pallas_call(handed_over, out_shape=[jax.ShapeDtypeStruct(r.shape, r.dt...  9.12 us

profile of v4, /device:TPU:22, one launch (start us, length us, event | category | flops | bytes accessed | tf_op | source)
XLA Modules:
  0.0 238.7 jit_solution(3044118730988289738)
XLA Ops:
  0.6 228.7 %step.1 = (bf16[2,512,1280]{2,1,0:T(8,128)(2,1)}, bf16[2,512,1280]{2,1,0:T(8,128)(2,1)}, bf16[2,1280,512]{2,1,0:T(8,128)(2,1)}, f32[2,64,1280]{2,1,0:T(8,128)}, ...) custom-call(bf16[1,4096,512]{2,1,0:T(8,128)(2,1)} %x_in.1, ...), custom_call_target="tpu_custom_call" | custom-call | tf_op jit(solution)/shard_map/step/pallas_call | solution.py:372
  229.4 9.1 %hand_over.1 = (bf16[2,512,1280]{2,1,0:T(8,128)(2,1)}, bf16[2,512,1280]{2,1,0:T(8,128)(2,1)}, bf16[2,1280,512]{2,1,0:T(8,128)(2,1)}, f32[2,64,1280]{2,1,0:T(8,12...) custom-call(bf16[2,512,1280]{2,1,0:T(8,128)(2,1)} %get-tuple-element, ...), custom_call_target="tpu_custom_call" | custom-call | tf_op jit(solution)/shard_map/hand_over/pallas_call | solution.py:435

commit v5 on v4

--- a/solution.py
+++ b/solution.py
@@ -12,7 +12,7 @@
 TF = 512
 TB = 1024
 SUBS = 4
-SETS = 4
+SETS = 5
 
 
 def dot(a, b):
@@ -42,7 +42,7 @@
     return jnp.concatenate([t[:, size * k : size * (k + 1)] for k in range(n) for t in blocks], 1)
 
 
-def forward(n, wg0, wu0, ready, x, dy, w, h, a2, a_t, dy_t, hid, da):
+def forward(n, ready, x, dy, w, h, a2, a_t, dy_t, hid, da):
     wg, wu, wd = w
     blocks = wg.shape[2] // FB
     share = wg.shape[1] // (x.shape[0] // TF)
@@ -67,8 +67,7 @@
         x[rows, :] = a
         da[rows, :] = jnp.zeros((TF, x.shape[1]), F32)
         some = pl.ds(pl.multiple_of(i * share, share), share)
-        for natural, new in zip((wg, wu), (wg0, wu0), strict=True):
-            new[some, :] = grouped(natural[0, some, :], n)
+        for natural in (wg, wu):
             natural[1, some, :] = grouped(natural[1, some, :], n)
         return 0
 
@@ -222,7 +221,7 @@
         for c in tokens(i):
             c.wait()
 
-    forward(n, wg0, wu0, ready, x, dy, w, h, a2, a_t, dy_t, hid, da)
+    forward(n, ready, x, dy, w, h, a2, a_t, dy_t, hid, da)
     load_grouped(0)
     grouped_loaded(1)
     pl.semaphore_wait(barrier, n - 1)
@@ -240,10 +239,10 @@
 
     def tick(p, i):
         at_tick(i, 0, p, 1, 0)
-        at_tick(i, 1, p, 2, 2)
-        at_tick(i, 1, p, 3, 4)
-        at_tick(i, 2, p, 1, 1)
-        at_tick(i, 3, p, 2, 3)
+        at_tick(i, 0, p, 4, 4)
+        at_tick(i, 1, p, 3, 3)
+        at_tick(i, 2, p, 2, 2)
+        at_tick(i, 3, p, 1, 1)
 
     da_all = da
 
@@ -275,6 +274,14 @@
 
     backward(1, 0, a2, da)
     grouped_loaded(0)
+
+    def regroup(i, _):
+        some = pl.ds(pl.multiple_of(i * per, per), per)
+        for natural, new in ((wg, wg0), (wu, wu0)):
+            new[some, :] = grouped(natural[0, some, :], n)
+        return 0
+
+    lax.fori_loop(0, n, regroup, 0)
     backward(0, blocks, x, None)
 
     def squares(p):
@@ -284,11 +291,9 @@
     local = jnp.float32(0)
     for s in range(n // 2 + 1):
         piece(end, s)
-        if s == 0:
-            piece(end - 1, 2)
-            piece(end - 2, 4)
-        elif s < 3:
-            piece(end - 1, s + 2)
+        if s < 3:
+            for back in range(1, 4 - s):
+                piece(end - back, s + 1 + back)
         elif s == 3:
             local += sum(squares(p) for p in range(end))
 

time: 239 us -> 241 us (level)
  no operation moved by 1% of the time
where the time goes in v5:
time: 241 us
  Pallas kernels  240 us (100%)
    pallas_call x1, Pallas kernels, stepped(): pl.pallas_call(functools.partial(kernel, n), out_shape=[jax.ShapeDtypeStr...  231 us
    pallas_call x1, Pallas kernels, both(): pl.pallas_call(handed_over, out_shape=[jax.ShapeDtypeStruct(r.shape, r.dt...  9.12 us

profile of v5, /device:TPU:22, one launch (start us, length us, event | category | flops | bytes accessed | tf_op | source)
XLA Modules:
  0.0 240.9 jit_solution(9568442326133787646)
XLA Ops:
  0.6 230.9 %step.1 = (bf16[2,512,1280]{2,1,0:T(8,128)(2,1)}, bf16[2,512,1280]{2,1,0:T(8,128)(2,1)}, bf16[2,1280,512]{2,1,0:T(8,128)(2,1)}, f32[2,64,1280]{2,1,0:T(8,128)}, ...) custom-call(bf16[1,4096,512]{2,1,0:T(8,128)(2,1)} %x_in.1, ...), custom_call_target="tpu_custom_call" | custom-call | tf_op jit(solution)/shard_map/step/pallas_call | solution.py:377
  231.6 9.1 %hand_over.1 = (bf16[2,512,1280]{2,1,0:T(8,128)(2,1)}, bf16[2,512,1280]{2,1,0:T(8,128)(2,1)}, bf16[2,1280,512]{2,1,0:T(8,128)(2,1)}, f32[2,64,1280]{2,1,0:T(8,12...) custom-call(bf16[2,512,1280]{2,1,0:T(8,128)(2,1)} %get-tuple-element, ...), custom_call_target="tpu_custom_call" | custom-call | tf_op jit(solution)/shard_map/hand_over/pallas_call | solution.py:440
